TPU v7x, 32 devices: a whole 2x2x4 slice. The times are simulated.
32 devices in a mesh: row: 4 (over y, x), col: 8 (over z, core).
Axes of the slice: x: 2, y: 2, z: 4, core: 2. Of those that a mesh axis runs over, the one named last changes fastest.
Arguments:
- e_field: float32 [3, 64, 32, 1024], P(None, None, 'row', 'col'), may hold values from -6 to 6
- h_field: float32 [3, 64, 32, 1024], P(None, None, 'row', 'col'), may hold values from -6 to 6
- e_coef: float32 [64, 32, 1024], P(None, 'row', 'col'), may hold values from 0.125 to 0.5
- basis: float32 [128, 32, 1024], P('row', None, 'col'), may hold values from -0.03125 to 0.03125
- pml_width: int32 [4], replicated, may hold values from 2 to 8
- snap_index: int32 [64], replicated, may hold values from 0 to 383
Outputs:
- e_final: float32 [3, 64, 32, 1024], P(None, None, 'row', 'col')
- h_final: float32 [3, 64, 32, 1024], P(None, None, 'row', 'col')
- coefficients: float32 [64, 128], replicated
- gram: float32 [64, 64], replicated
All inputs are finite; a program needn't handle non-finite values.
Results may differ from a plain program's by a relative error of at most 0.00008.
Values sent between devices are 32-bit elements; how exact they have to be, the bound alone decides.
A program may use at most 64 MiB of HBM per device.

v0:
```python
import functools
import jax
import jax.numpy as jnp
from jax import lax
from jax.experimental import pallas as pl
from jax.experimental.pallas import tpu as pltpu
from jax.sharding import PartitionSpec as P

STEPS = 8
UNROLL = 16

time_step = 0.5
sigma_top = 4.0
alpha_shift = 0.05


def absorber(positions, total, low, high):
    depth = jnp.maximum(
        jnp.maximum((low - positions) / low, (positions - (total - 1.0 - high)) / high), 0.0
    )
    sigma = sigma_top * (depth * depth * depth)
    damp = jnp.exp(-(sigma + alpha_shift) * time_step)
    gain = sigma / (sigma + alpha_shift) * (damp - 1.0)
    return damp, gain


def step_kernel(
    n_row, n_col, width_ref, index_ref, e_in, h_in, coef_in, basis_in, e_out, h_out, proj_out, gram_out,
    fields, coef_s, psi, first_x, last_x, h_last_x, first_y, last_y, h_last_y,
    next_x, prev_x, halo_x, halo_psi_x, next_y, prev_y, corner_x, corner_y, halo_y, halo_psi_y,
    prof, modes, snaps, part, row_sums, col_sums, total,
    local_sem, x_send, x_recv, send_sem, recv_sem, once_send, once_recv, mode_send, mode_recv,
    sum_send, sum_recv, col_send, col_recv, back_send, back_recv,
):
    e_s, h_s = fields.at[pl.ds(0, 3)], fields.at[pl.ds(3, 3)]
    nz, nx, ny = coef_s.shape
    row, col = lax.axis_index("row"), lax.axis_index("col")
    up, down = row > 0, row < n_row - 1
    left, right = col > 0, col < n_col - 1
    sw = jnp.logical_and(down, left)
    ne = jnp.logical_and(up, right)
    routes = (
        (up, {"row": row - 1, "col": col}), (down, {"row": row + 1, "col": col}),
        (left, {"row": row, "col": col - 1}), (sw, {"row": row + 1, "col": col - 1}),
        (right, {"row": row, "col": col + 1}), (ne, {"row": row - 1, "col": col + 1}),
        (left, {"row": row, "col": col - 1}),
    )
    chunks = nz // UNROLL
    half = chunks // 2

    load_e = pltpu.make_async_copy(e_in, e_s.at[:, pl.ds(0, nz)], local_sem.at[0])
    load_h = pltpu.make_async_copy(h_in, h_s.at[:, pl.ds(1, nz)], local_sem.at[1])
    load_c = pltpu.make_async_copy(coef_in, coef_s, local_sem.at[2])
    load_e.start()
    load_h.start()
    load_c.start()
    n_modes = basis_in.shape[0]
    modes_3d = modes.reshape(n_modes * n_row, nx, ny)
    load_b = pltpu.make_async_copy(
        basis_in.at[:, pl.ds(pl.multiple_of(row * nx, nx), nx)],
        modes_3d.at[pl.ds(row * n_modes, n_modes)], local_sem.at[3])
    load_b.start()
    row_peers = [lax.rem(row + k, n_row) for k in range(1, n_row)]
    col_peers = [lax.rem(col + k, n_col) for k in range(1, n_col)]

    part[...] = jnp.zeros_like(part)
    next_x[...] = jnp.zeros_like(next_x)
    prev_x[...] = jnp.zeros_like(prev_x)
    halo_x[...] = jnp.zeros_like(halo_x)
    halo_psi_x[...] = jnp.zeros_like(halo_psi_x)
    next_y[...] = jnp.zeros_like(next_y)
    prev_y[...] = jnp.zeros_like(prev_y)
    corner_x[...] = jnp.zeros_like(corner_x)
    corner_y[...] = jnp.zeros_like(corner_y)
    halo_y[...] = jnp.zeros_like(halo_y)
    halo_psi_y[...] = jnp.zeros_like(halo_psi_y)

    barrier = pltpu.get_barrier_semaphore()
    for peer in row_peers:
        pl.semaphore_signal(
            barrier, inc=1, device_id={"row": peer, "col": col}, device_id_type=pl.DeviceIdType.MESH)
    for peer in col_peers:
        pl.semaphore_signal(
            barrier, inc=1, device_id={"row": row, "col": peer}, device_id_type=pl.DeviceIdType.MESH)
    for m in (3, 5):
        @pl.when(routes[m][0])
        def _():
            pl.semaphore_signal(
                barrier, inc=1, device_id=routes[m][1], device_id_type=pl.DeviceIdType.MESH)

    zero = jnp.zeros((nx, ny), jnp.float32)
    for c in range(3):
        e_s[c, nz] = zero
        h_s[c, 0] = zero

    def clear(z, carry):
        for k in range(8):
            psi[k, z] = zero
        return carry

    lax.fori_loop(0, nz, clear, 0)

    sub = lax.broadcasted_iota(jnp.int32, (nx, ny), 0)
    lane = lax.broadcasted_iota(jnp.int32, (nx, ny), 1)
    w = [jnp.full((nx, ny), width_ref[k], jnp.int32).astype(jnp.float32) for k in range(4)]
    x_pos = (sub + row * nx).astype(jnp.float32)
    y_pos = (lane + col * ny).astype(jnp.float32)
    x_before = (jnp.zeros_like(sub) + (row * nx - 1)).astype(jnp.float32)
    y_before = (jnp.zeros_like(sub) + (col * ny - 1)).astype(jnp.float32)
    full_x, full_y = float(nx * n_row), float(ny * n_col)
    pairs = (
        absorber(x_pos + 0.5, full_x, w[0], w[1]), absorber(y_pos + 0.5, full_y, w[2], w[3]),
        absorber(x_pos, full_x, w[0], w[1]), absorber(y_pos, full_y, w[2], w[3]),
        absorber(x_before + 0.5, full_x, w[0], w[1]), absorber(y_before + 0.5, full_y, w[2], w[3]),
    )
    for k, (damp, gain) in enumerate(pairs):
        prof[2 * k] = damp
        prof[2 * k + 1] = gain

    def pack(z, ex, ey, ez, cols):
        first, last0, last1 = cols
        first_x[0, pl.ds(z, 1), :] = ey[0:1]
        first_x[1, pl.ds(z, 1), :] = ez[0:1]
        last_x[0, pl.ds(z, 1), :] = ex[nx - 1:nx]
        last_x[1, pl.ds(z, 1), :] = ey[nx - 1:nx]
        last_x[2, pl.ds(z, 1), :] = ez[nx - 1:nx]
        rx = pltpu.roll(ex, z, 1)
        rz = pltpu.roll(ez, z + nz, 1)
        ry = pltpu.roll(ey, z, 1)
        first = jnp.where(lane == z, rx, jnp.where(lane == z + nz, rz, first))
        before = lax.rem(z + ny - 1, ny)
        last0 = jnp.where(lane == before, rx, jnp.where(lane == z + nz - 1, rz, last0))
        last1 = jnp.where(lane == before, ry, last1)
        return first, last0, last1

    def keep(cols):
        first_y[1] = cols[0]
        last_y[0] = pltpu.roll(cols[1], 1, 1)
        last_y[1] = pltpu.roll(cols[2], 1, 1)

    def remote(m, src, dst, send, recv):
        return pltpu.make_async_remote_copy(
            src_ref=src, dst_ref=dst, send_sem=send, recv_sem=recv,
            device_id=routes[m][1], device_id_type=pl.DeviceIdType.MESH)

    def copy_of(m, slot, k=None):
        if m < 2:
            here = pl.ds(pl.multiple_of(k * UNROLL, UNROLL), UNROLL)
            src, dst = ((first_x, next_x), (last_x, prev_x))[m]
            return remote(
                m, src.at[:, here], dst.at[slot, :, here], x_send.at[m, slot, k], x_recv.at[m, slot, k])
        src, dst = {
            2: (first_y.at[1], next_y.at[slot, 1]), 3: (first_y.at[1], corner_x.at[slot]),
            4: (last_y, prev_y.at[slot]), 5: (last_y.at[1], corner_y.at[slot]),
            6: (first_y.at[0], next_y.at[slot, 0]),
        }[m]
        return remote(m, src, dst, send_sem.at[m, slot], recv_sem.at[m, slot])

    def start(m, slot, k=None):
        @pl.when(routes[m][0])
        def _():
            copy_of(m, slot, k).start()

    arrives = (down, up, right, ne, left, sw, right)

    def wait_recv(m, slot, k=None):
        @pl.when(arrives[m])
        def _():
            copy_of(m, slot, k).wait_recv()

    def wait_send(m, slot, k=None):
        @pl.when(routes[m][0])
        def _():
            copy_of(m, slot, k).wait_send()

    load_e.wait()
    load_h.wait()

    def first_pack(k, carry):
        cols, hcol = carry
        for j in range(UNROLL):
            z = k * UNROLL + j
            cols = pack(z, e_s[0, z], e_s[1, z], e_s[2, z], cols)
            hx, hy, hz = h_s[0, z + 1], h_s[1, z + 1], h_s[2, z + 1]
            h_last_x[0, pl.ds(z, 1), :] = hy[nx - 1:nx]
            h_last_x[1, pl.ds(z, 1), :] = hz[nx - 1:nx]
            hcol = jnp.where(lane == z, pltpu.roll(hz, z + 1, 1), hcol)
            hcol = jnp.where(lane == z + nz, pltpu.roll(hx, lax.rem(z + nz + 1, ny), 1), hcol)
        return cols, hcol

    cols, hcol = lax.fori_loop(0, nz // UNROLL, first_pack, ((zero, zero, zero), zero))
    keep(cols)
    first_y[0] = cols[0]
    h_last_y[...] = hcol

    count = n_row - 1 + n_col - 1 + sw.astype(jnp.int32) + ne.astype(jnp.int32)
    pl.semaphore_wait(barrier, count)
    once = [
        pltpu.make_async_remote_copy(
            src_ref=src, dst_ref=dst, send_sem=once_send.at[k], recv_sem=once_recv.at[k],
            device_id=routes[m][1], device_id_type=pl.DeviceIdType.MESH)
        for k, (src, dst, m) in enumerate(((h_last_x, halo_x, 1), (h_last_y, halo_y, 4)))
    ]
    for k in range(chunks):
        start(0, 0, k)
        start(1, 0, k)
    for m in (2, 4, 6, 3, 5):
        start(m, 0)
    for k, m in enumerate((1, 4)):
        @pl.when(routes[m][0])
        def _():
            once[k].start()
    load_c.wait()
    piece = n_modes // STEPS

    def mode_copies(s):
        return [
            pltpu.make_async_remote_copy(
                src_ref=basis_in.at[pl.ds(s * piece, piece), pl.ds(pl.multiple_of(peer * nx, nx), nx)],
                dst_ref=modes_3d.at[pl.ds(row * n_modes + s * piece, piece)],
                send_sem=mode_send.at[k, s], recv_sem=mode_recv.at[k, s],
                device_id={"row": peer, "col": col}, device_id_type=pl.DeviceIdType.MESH)
            for k, peer in enumerate(row_peers)
        ]

    def magnetic(slot):
        hdx, hgx, hdy, hgy = prof[0], prof[1], prof[2], prof[3]

        def body(k, carry):
            wait_recv(0, slot, k)

            @pl.when(k == 0)
            def _():
                wait_recv(6, slot)

            @pl.when(k == half)
            def _():
                wait_recv(2, slot)

            edge = next_y[slot, k // half]
            for j in range(UNROLL):
                z = k * UNROLL + j
                ex, ey, ez = e_s[0, z], e_s[1, z], e_s[2, z]
                row_y = jnp.broadcast_to(next_x[slot, 0, pl.ds(z, 1), :], (nx, ny))
                row_z = jnp.broadcast_to(next_x[slot, 1, pl.ds(z, 1), :], (nx, ny))
                col_x = pltpu.roll(edge, ny - 1 - z, 1)
                col_z = pltpu.roll(edge, ny - 1 - nz - z, 1)
                ey_dz = e_s[1, z + 1] - ey
                ex_dz = e_s[0, z + 1] - ex
                ez_dy = jnp.where(lane == ny - 1, col_z, pltpu.roll(ez, ny - 1, 1)) - ez
                ex_dy = jnp.where(lane == ny - 1, col_x, pltpu.roll(ex, ny - 1, 1)) - ex
                ez_dx = jnp.where(sub == nx - 1, row_z, pltpu.roll(ez, nx - 1, 0)) - ez
                ey_dx = jnp.where(sub == nx - 1, row_y, pltpu.roll(ey, nx - 1, 0)) - ey
                p0 = hdy * psi[0, z] + hgy * ez_dy
                p1 = hdx * psi[1, z] + hgx * ez_dx
                p2 = hdx * psi[2, z] + hgx * ey_dx
                p3 = hdy * psi[3, z] + hgy * ex_dy
                psi[0, z], psi[1, z], psi[2, z], psi[3, z] = p0, p1, p2, p3
                h_s[0, z + 1] = h_s[0, z + 1] - time_step * (ez_dy + p0 - ey_dz)
                h_s[1, z + 1] = h_s[1, z + 1] - time_step * (ex_dz - ez_dx - p1)
                h_s[2, z + 1] = h_s[2, z + 1] - time_step * (ey_dx + p2 - ex_dy - p3)
            return carry

        lax.fori_loop(0, nz // UNROLL, body, 0)

    def magnetic_row_before(slot):
        hdy, hgy = prof[2][0:1], prof[3][0:1]
        hdx, hgx = prof[8][0:1], prof[9][0:1]
        ex, ey, ez = prev_x[slot, 0, 0:nz], prev_x[slot, 1, 0:nz], prev_x[slot, 2, 0:nz]
        big_lane = lax.broadcasted_iota(jnp.int32, (nz, ny), 1)
        big_z = lax.broadcasted_iota(jnp.int32, (nz, ny), 0)
        corner = jnp.broadcast_to(corner_x[slot, nx - 1:nx, :], (nz, ny))
        corner = jnp.sum(jnp.where(big_lane == big_z, corner, 0.0), axis=1, keepdims=True)
        ex_dz = prev_x[slot, 0, 1:nz + 1] - ex
        ex_dy = jnp.where(big_lane == ny - 1, corner, pltpu.roll(ex, ny - 1, 1)) - ex
        ey_dx = first_x[0] - ey
        ez_dx = first_x[1] - ez
        p1 = hdx * halo_psi_x[0] + hgx * ez_dx
        p2 = hdx * halo_psi_x[1] + hgx * ey_dx
        p3 = hdy * halo_psi_x[2] + hgy * ex_dy
        halo_psi_x[0], halo_psi_x[1], halo_psi_x[2] = p1, p2, p3
        mask = up.astype(jnp.float32)
        halo_x[0] = mask * (halo_x[0] - time_step * (ex_dz - ez_dx - p1))
        halo_x[1] = mask * (halo_x[1] - time_step * (ey_dx + p2 - ex_dy - p3))

    def magnetic_column_before(slot):
        hdx, hgx = prof[0], prof[1]
        hdy, hgy = prof[10], prof[11]
        ey = prev_y[slot, 1]
        dy = first_y[1] - prev_y[slot, 0]
        below = jnp.broadcast_to(corner_y[slot, 0:1, :], (nx, ny))
        ey_dx = jnp.where(sub == nx - 1, below, pltpu.roll(ey, nx - 1, 0)) - ey
        ey_dz = pltpu.roll(pltpu.roll(ey, ny - 1, 1) - ey, nz, 1)
        py = hdy * halo_psi_y[0] + hgy * dy
        px = hdx * halo_psi_y[1] + hgx * ey_dx
        halo_psi_y[0], halo_psi_y[1] = py, px
        mask = left.astype(jnp.float32)
        change = jnp.where(lane < nz, ey_dx + px - dy - py, dy + py - ey_dz)
        halo_y[...] = mask * (halo_y[...] - time_step * change)

    def electric(s, slot):
        edx, egx, edy, egy = prof[4], prof[5], prof[6], prof[7]
        edge = halo_y[...]

        def body(k, cols):
            for j in range(UNROLL):
                z = k * UNROLL + j
                hx, hy, hz = h_s[0, z + 1], h_s[1, z + 1], h_s[2, z + 1]
                row_y = jnp.broadcast_to(halo_x[0, pl.ds(z, 1), :], (nx, ny))
                row_z = jnp.broadcast_to(halo_x[1, pl.ds(z, 1), :], (nx, ny))
                col_z = pltpu.roll(edge, lax.rem(ny - z, ny), 1)
                col_x = pltpu.roll(edge, ny - nz - z, 1)
                hy_dz = hy - h_s[1, z]
                hx_dz = hx - h_s[0, z]
                hz_dy = hz - jnp.where(lane == 0, col_z, pltpu.roll(hz, 1, 1))
                hx_dy = hx - jnp.where(lane == 0, col_x, pltpu.roll(hx, 1, 1))
                hz_dx = hz - jnp.where(sub == 0, row_z, pltpu.roll(hz, 1, 0))
                hy_dx = hy - jnp.where(sub == 0, row_y, pltpu.roll(hy, 1, 0))
                p0 = edy * psi[4, z] + egy * hz_dy
                p1 = edx * psi[5, z] + egx * hz_dx
                p2 = edx * psi[6, z] + egx * hy_dx
                p3 = edy * psi[7, z] + egy * hx_dy
                psi[4, z], psi[5, z], psi[6, z], psi[7, z] = p0, p1, p2, p3
                amount = coef_s[z]
                ex = e_s[0, z] + amount * (hz_dy + p0 - hy_dz)
                ey = e_s[1, z] + amount * (hx_dz - hz_dx - p1)
                ez = e_s[2, z] + amount * (hy_dx + p2 - hx_dy - p3)
                e_s[0, z], e_s[1, z], e_s[2, z] = ex, ey, ez
                cols = pack(z, ex, ey, ez, cols)
            more = s < STEPS - 1

            @pl.when(more)
            def _():
                start(0, slot, k)
                start(1, slot, k)

            @pl.when(k == half - 1)
            def _():
                first_y[0] = cols[0]

                @pl.when(more)
                def _():
                    start(6, slot)

            return cols

        keep(lax.fori_loop(0, nz // UNROLL, body, (zero, zero, zero)))

    def step(s, carry):
        slot = lax.rem(s, 2)
        for copy in mode_copies(s):
            copy.start()
        magnetic(slot)
        for k in range(chunks):
            wait_recv(1, slot, k)
        wait_recv(3, slot)

        @pl.when(s == 0)
        def _():
            for k, there in enumerate((up, left)):
                @pl.when(there)
                def _():
                    once[k].wait_recv()

        magnetic_row_before(slot)
        wait_recv(4, slot)
        wait_recv(5, slot)
        magnetic_column_before(slot)
        for k in range(chunks):
            wait_send(0, slot, k)
            wait_send(1, slot, k)
        for m in range(2, 7):
            wait_send(m, slot)
        electric(s, 1 - slot)

        @pl.when(s < STEPS - 1)
        def _():
            for m in (2, 4, 3, 5):
                start(m, 1 - slot)

        return carry

    lax.fori_loop(0, STEPS, step, 0)
    for k, m in enumerate((1, 4)):
        @pl.when(routes[m][0])
        def _():
            once[k].wait_send()
    store_e = pltpu.make_async_copy(e_s.at[:, pl.ds(0, nz)], e_out, local_sem.at[0])
    store_h = pltpu.make_async_copy(h_s.at[:, pl.ds(1, nz)], h_out, local_sem.at[1])
    store_e.start()
    store_h.start()

    count = snaps.shape[0] // nx

    def pick(s, carry):
        planes = []
        for j in range(8):
            index = index_ref[s * 8 + j]
            c = index // nz
            planes.append(fields[c, index - c * nz + (c // 3)])
        for j in range(8):
            snaps[pl.ds(pl.multiple_of((s * 8 + j) * nx, nx), nx), :] = planes[j]
        return carry

    lax.fori_loop(0, count // 8, pick, 0)
    load_b.wait()

    def wait_modes(s, carry):
        for copy in mode_copies(s):
            copy.wait()
        return carry

    lax.fori_loop(0, STEPS, wait_modes, 0)
    n_all = modes.shape[0] // nx
    dims = (((1,), (1,)), ((), ()))
    proj, gram = None, None
    for x in range(nx):
        a = snaps[pl.ds(x, count, stride=nx), :]
        b = modes[pl.ds(x, n_all, stride=nx), :]
        p = lax.dot_general(a, b, dims, precision=lax.Precision.HIGHEST, preferred_element_type=jnp.float32)
        g = lax.dot_general(a, a, dims, precision=lax.Precision.HIGHEST, preferred_element_type=jnp.float32)
        proj, gram = (p, g) if x == 0 else (proj + p, gram + g)
    part[:, 0:n_all] = proj
    part[:, n_all:n_all + count] = gram / float(nx * n_row * ny * n_col)

    share = count // n_row
    own = pl.ds(pl.multiple_of(row * share, share), share)

    def exchange(peers, axis, src_of, dst, sends, recvs):
        result = []
        for k, peer in enumerate(peers):
            where = {"row": row, "col": col}
            where[axis] = peer
            result.append(pltpu.make_async_remote_copy(
                src_ref=src_of(peer), dst_ref=dst, send_sem=sends.at[k], recv_sem=recvs.at[k],
                device_id=where, device_id_type=pl.DeviceIdType.MESH))
        for copy in result:
            copy.start()
        for copy in result:
            copy.wait()

    row_sums[row] = part[own, :]
    exchange(
        row_peers, "row", lambda peer: part.at[pl.ds(pl.multiple_of(peer * share, share), share)],
        row_sums.at[row], sum_send, sum_recv)
    value = row_sums[0]
    for k in range(1, n_row):
        value = value + row_sums[k]
    col_sums[col] = value
    exchange(col_peers, "col", lambda peer: col_sums.at[col], col_sums.at[col], col_send, col_recv)
    value = col_sums[0]
    for k in range(1, n_col):
        value = value + col_sums[k]
    total[own, :] = value
    exchange(row_peers, "row", lambda peer: total.at[own], total.at[own], back_send, back_recv)
    proj_out[...] = total[:, 0:n_all]
    gram_out[...] = total[:, n_all:n_all + count]
    store_e.wait()
    store_h.wait()


def shards(e_field, h_field, e_coef, basis, pml_width, snap_index):
    nz, nx, ny = e_coef.shape
    n_row, n_col = lax.axis_size("row"), lax.axis_size("col")
    modes, count = basis.shape[0] * n_row, snap_index.shape[0]
    f32 = jnp.float32
    wide = modes + (count + 127) // 128 * 128
    any_space = pl.BlockSpec(memory_space=pl.ANY)
    smem, vmem = pl.BlockSpec(memory_space=pltpu.SMEM), pl.BlockSpec(memory_space=pltpu.VMEM)
    return pl.pallas_call(
        functools.partial(step_kernel, n_row, n_col),
        out_shape=[
            jax.ShapeDtypeStruct(e_field.shape, f32), jax.ShapeDtypeStruct(h_field.shape, f32),
            jax.ShapeDtypeStruct((count, modes), f32), jax.ShapeDtypeStruct((count, count), f32),
        ],
        in_specs=[smem, smem, any_space, any_space, any_space, any_space],
        out_specs=[any_space, any_space, vmem, vmem],
        scratch_shapes=[
            pltpu.VMEM((6, nz + 1, nx, ny), f32),
            pltpu.VMEM((nz, nx, ny), f32), pltpu.VMEM((8, nz, nx, ny), f32),
            pltpu.VMEM((2, nz, ny), f32), pltpu.VMEM((3, nz, ny), f32), pltpu.VMEM((2, nz, ny), f32),
            pltpu.VMEM((2, nx, ny), f32), pltpu.VMEM((2, nx, ny), f32), pltpu.VMEM((nx, ny), f32),
            pltpu.VMEM((2, 2, nz, ny), f32), pltpu.VMEM((2, 3, nz + 8, ny), f32),
            pltpu.VMEM((2, nz, ny), f32), pltpu.VMEM((3, nz, ny), f32),
            pltpu.VMEM((2, 2, nx, ny), f32), pltpu.VMEM((2, 2, nx, ny), f32),
            pltpu.VMEM((2, nx, ny), f32), pltpu.VMEM((2, nx, ny), f32),
            pltpu.VMEM((nx, ny), f32), pltpu.VMEM((2, nx, ny), f32),
            pltpu.VMEM((12, nx, ny), f32),
            pltpu.VMEM((modes * nx, ny), f32), pltpu.VMEM((count * nx, ny), f32),
            pltpu.VMEM((count, wide), f32), pltpu.VMEM((n_row, count // n_row, wide), f32),
            pltpu.VMEM((n_col, count // n_row, wide), f32), pltpu.VMEM((count, wide), f32),
            pltpu.SemaphoreType.DMA((4,)),
            pltpu.SemaphoreType.DMA((2, 2, nz // UNROLL)), pltpu.SemaphoreType.DMA((2, 2, nz // UNROLL)),
            pltpu.SemaphoreType.DMA((7, 2)), pltpu.SemaphoreType.DMA((7, 2)),
            pltpu.SemaphoreType.DMA((2,)), pltpu.SemaphoreType.DMA((2,)),
            pltpu.SemaphoreType.DMA((n_row - 1, STEPS)), pltpu.SemaphoreType.DMA((n_row - 1, STEPS)),
            pltpu.SemaphoreType.DMA((n_row - 1,)), pltpu.SemaphoreType.DMA((n_row - 1,)),
            pltpu.SemaphoreType.DMA((n_col - 1,)), pltpu.SemaphoreType.DMA((n_col - 1,)),
            pltpu.SemaphoreType.DMA((n_row - 1,)), pltpu.SemaphoreType.DMA((n_row - 1,)),
        ],
        compiler_params=pltpu.CompilerParams(
            collective_id=0, has_side_effects=True, vmem_limit_bytes=67_043_328
        ),
    )(pml_width, snap_index, e_field, h_field, e_coef, basis)


def solution(mesh):
    in_specs = (
        P(None, None, "row", "col"),
        P(None, None, "row", "col"),
        P(None, "row", "col"),
        P("row", None, "col"),
        P(),
        P(),
    )
    out_specs = (P(None, None, "row", "col"), P(None, None, "row", "col"), P(), P())
    return jax.shard_map(shards, mesh=mesh, in_specs=in_specs, out_specs=out_specs, check_vma=False)
```

profile of v0, /device:TPU:0, one launch (start us, length us, event | category | flops | bytes accessed | tf_op | source)
XLA Modules:
  0.0 76.6 jit_solution(6170011844363688621)
XLA Ops:
  0.6 71.6 %shard_map.93 = (f32[3,64,8,128]{3,2,1,0:T(8,128)}, f32[3,64,8,128]{3,2,1,0:T(8,128)}, f32[64,128]{1,0:T(8,128)}, f32[64,64]{1,0:T(8,128)}) custom-call(s32[4]{0:T(128)} %width_ref.1, s32[64]{0:T(128)} %index_ref.1, f32[3,64,8,128]{3,2,1,0:T(8,128)} %e_in.1, f32[3,64,8,128]{3,2,1,0:T(8,128)} %h_in.1, f32[64,8,128]{2,1,0:T(8,128)} %coef_in.1, ...), custom_call_target="tpu_custom_call" | custom-call | tf_op jit(solution)/shard_map/pallas_call | solution.py:470
  72.2 0.0 copy-start
  72.2 2.1 %copy.14 = f32[3,64,8,128]{3,2,1,0:T(8,128)} copy(f32[3,64,8,128]{3,2,1,0:T(8,128)} %get-tuple-element.8) | data formatting | bytes 1572864
  74.3 0.0 copy-done
  74.3 0.0 copy-start.2
  74.3 0.9 %copy.15 = f32[3,64,8,128]{3,2,1,0:T(8,128)} copy(f32[3,64,8,128]{3,2,1,0:T(8,128)S(1)} %copy-done) | data formatting | bytes 1572864
  75.2 0.0 copy-done.2
  75.2 0.0 copy-start.1
  75.2 0.6 copy.16
  75.8 0.2 copy-done.1
  76.0 0.6 copy.17
Async XLA Ops:
  72.2 2.1 %copy-start = (f32[3,64,8,128]{3,2,1,0:T(8,128)S(1)}, f32[3,64,8,128]{3,2,1,0:T(8,128)}, u32[]{:S(2)}) copy-start(f32[3,64,8,128]{3,2,1,0:T(8,128)} %get-tuple-element.9) | copy-start | bytes 2359300
  74.3 0.9 %copy-start.2 = (f32[64,128]{1,0:T(8,128)S(1)}, f32[64,128]{1,0:T(8,128)}, u32[]{:S(2)}) copy-start(f32[64,128]{1,0:T(8,128)} %get-tuple-element.10) | copy-start | bytes 98308
  75.2 0.8 %copy-start.1 = (f32[64,64]{1,0:T(8,128)S(1)}, f32[64,64]{1,0:T(8,128)}, u32[]{:S(2)}) copy-start(f32[64,64]{1,0:T(8,128)} %get-tuple-element.11) | copy-start | bytes 49156
where the time goes:
time: 76.9 us; the launch traced here: 76.6 us
  Pallas kernels  71.6 us (93%)
  local copies, waits for them, and re-layouts  4.41 us (6%)
    pallas_call x1, Pallas kernels, shards(): pl.pallas_call(functools.partial(step_kernel, n_row, n_col), out_shape=[j...  71.6 us
    unnamed x10, local copies, waits for them, and re-layouts  4.41 us

commit v1 on v0

v1 whole, which is shorter than its diff:
```python
import functools
import jax
import jax.numpy as jnp
from jax import lax
from jax.experimental import pallas as pl
from jax.experimental.pallas import tpu as pltpu
from jax.sharding import PartitionSpec as P

STEPS = 8

time_step = 0.5
sigma_top = 4.0
alpha_shift = 0.05


def absorber(positions, total, low, high):
    depth = jnp.maximum(
        jnp.maximum((low - positions) / low, (positions - (total - 1.0 - high)) / high), 0.0
    )
    sigma = sigma_top * (depth * depth * depth)
    damp = jnp.exp(-(sigma + alpha_shift) * time_step)
    gain = sigma / (sigma + alpha_shift) * (damp - 1.0)
    return damp, gain


def step_kernel(
    n_row, n_col, width_ref, index_ref, e_in, h_in, coef_in, basis_in, e_out, h_out, proj_out, gram_out,
    fields, coef_s, psi, side_e, side_h, side_coef, side_psi, first_y, y_out, y_in,
    up_out, up_in, down_out, down_in, last_x, row_psi, before, before_psi, before_h,
    prof, modes, snaps, part, row_sums, col_sums, total,
    local_sem, y_send, y_recv, x_send, x_recv, mode_send, mode_recv,
    sum_send, sum_recv, col_send, col_recv, back_send, back_recv,
):
    e_s, h_s = fields.at[pl.ds(0, 3)], fields.at[pl.ds(3, 3)]
    nz, nx, ny = coef_s.shape
    width = STEPS
    group = ny // width
    size = group // 2
    chunks = nz // size
    half = ny // 2
    row, col = lax.axis_index("row"), lax.axis_index("col")
    up, down = row > 0, row < n_row - 1
    left, right = col > 0, col < n_col - 1

    load_e = pltpu.make_async_copy(e_in, e_s.at[:, pl.ds(0, nz)], local_sem.at[0])
    load_h = pltpu.make_async_copy(h_in, h_s.at[:, pl.ds(1, nz)], local_sem.at[1])
    load_c = pltpu.make_async_copy(coef_in, coef_s, local_sem.at[2])
    load_e.start()
    load_h.start()
    load_c.start()
    n_modes = basis_in.shape[0]
    modes_3d = modes.reshape(n_modes * n_row, nx, ny)
    load_b = pltpu.make_async_copy(
        basis_in.at[:, pl.ds(pl.multiple_of(row * nx, nx), nx)],
        modes_3d.at[pl.ds(row * n_modes, n_modes)], local_sem.at[3])
    load_b.start()
    row_peers = [lax.rem(row + k, n_row) for k in range(1, n_row)]
    col_peers = [lax.rem(col + k, n_col) for k in range(1, n_col)]

    part[...] = jnp.zeros_like(part)
    up_in[...] = jnp.zeros_like(up_in)
    down_in[...] = jnp.zeros_like(down_in)
    for side, there in enumerate((left, right)):
        @pl.when(jnp.logical_not(there))
        def _():
            y_in[side] = jnp.zeros(y_in.shape[1:], jnp.float32)

    barrier = pltpu.get_barrier_semaphore()
    for peer in row_peers:
        pl.semaphore_signal(
            barrier, inc=1, device_id={"row": peer, "col": col}, device_id_type=pl.DeviceIdType.MESH)
    for peer in col_peers:
        pl.semaphore_signal(
            barrier, inc=1, device_id={"row": row, "col": peer}, device_id_type=pl.DeviceIdType.MESH)

    zero = jnp.zeros((nx, ny), jnp.float32)
    for c in range(3):
        e_s[c, nz] = zero
        h_s[c, 0] = zero
        side_e[c, chunks] = zero
        side_h[c, 0] = zero
    last_x[0, chunks] = zero

    def clear(z, carry):
        for k in range(8):
            psi[k, z] = zero
        return carry

    lax.fori_loop(0, nz, clear, 0)
    side_psi[...] = jnp.zeros_like(side_psi)
    row_psi[...] = jnp.zeros_like(row_psi)
    before[...] = jnp.zeros_like(before)
    before_psi[...] = jnp.zeros_like(before_psi)

    sub = lax.broadcasted_iota(jnp.int32, (nx, ny), 0)
    lane = lax.broadcasted_iota(jnp.int32, (nx, ny), 1)
    spot = lax.rem(lane, width)
    block = lax.div(lax.rem(lane, half), width)
    on_left = lane < half
    w = [jnp.full((nx, ny), width_ref[k], jnp.int32).astype(jnp.float32) for k in range(4)]
    x_pos = (sub + row * nx).astype(jnp.float32)
    y_pos = (lane + col * ny).astype(jnp.float32)
    x_before = (jnp.zeros_like(sub) + (row * nx - 1)).astype(jnp.float32)
    x_last = (jnp.zeros_like(sub) + (row * nx + nx - 1)).astype(jnp.float32)
    y_side = (spot + col * ny + jnp.where(on_left, -width, ny)).astype(jnp.float32)
    full_x, full_y = float(nx * n_row), float(ny * n_col)
    pairs = (
        absorber(x_pos + 0.5, full_x, w[0], w[1]), absorber(y_pos + 0.5, full_y, w[2], w[3]),
        absorber(x_pos, full_x, w[0], w[1]), absorber(y_pos, full_y, w[2], w[3]),
        absorber(x_before + 0.5, full_x, w[0], w[1]), absorber(x_last + 0.5, full_x, w[0], w[1]),
        absorber(y_side + 0.5, full_y, w[2], w[3]), absorber(y_side, full_y, w[2], w[3]),
    )
    for k, (damp, gain) in enumerate(pairs):
        prof[2 * k] = damp
        prof[2 * k + 1] = gain
    side_step = time_step * jnp.where(on_left, left.astype(jnp.float32), right.astype(jnp.float32))
    up_mask = up.astype(jnp.float32)

    routes = ((up, {"row": row - 1, "col": col}), (down, {"row": row + 1, "col": col}))
    arrives = (down, up)
    rows = 2 * size + 2

    def copy_of(m, slot, k):
        src, dst = ((up_out, up_in), (down_out, down_in))[m]
        return pltpu.make_async_remote_copy(
            src_ref=src.at[k, pl.ds(0, rows)], dst_ref=dst.at[slot, k, pl.ds(0, rows)],
            send_sem=x_send.at[m, slot, k], recv_sem=x_recv.at[m, slot, k],
            device_id=routes[m][1], device_id_type=pl.DeviceIdType.MESH)

    def start(m, slot, k):
        @pl.when(routes[m][0])
        def _():
            copy_of(m, slot, k).start()

    def wait_recv(m, slot, k):
        @pl.when(arrives[m])
        def _():
            copy_of(m, slot, k).wait_recv()

    def wait_send(m, slot, k):
        @pl.when(routes[m][0])
        def _():
            copy_of(m, slot, k).wait_send()

    sides = ((left, {"row": row, "col": col - 1}), (right, {"row": row, "col": col + 1}))

    def y_copy(side):
        return pltpu.make_async_remote_copy(
            src_ref=y_out.at[side], dst_ref=y_in.at[1 - side], send_sem=y_send.at[side],
            recv_sem=y_recv.at[1 - side], device_id=sides[side][1], device_id_type=pl.DeviceIdType.MESH)

    def y_arrival(side):
        return pltpu.make_async_remote_copy(
            src_ref=y_out.at[1 - side], dst_ref=y_in.at[side], send_sem=y_send.at[1 - side],
            recv_sem=y_recv.at[side], device_id=sides[side][1], device_id_type=pl.DeviceIdType.MESH)

    load_e.wait()
    load_h.wait()
    load_c.wait()

    def plane(c, z):
        return e_s[c, z] if c < 3 else h_s[c - 3, z + 1] if c < 6 else coef_s[z]

    def pack_sides(q, carry):
        for c in range(7):
            first, last = zero, zero
            for i in range(group):
                value = plane(c, q * group + i)
                here = lax.div(lane, width) == i
                first = jnp.where(here, pltpu.roll(value, i * width, 1) if i else value, first)
                last = jnp.where(here, pltpu.roll(value, (i * width + width) % ny, 1) if (i + 1) % group else value, last)
            y_out[0, c, q] = first
            y_out[1, c, q] = last
        return carry

    lax.fori_loop(0, nz // group, pack_sides, 0)
    pl.semaphore_wait(barrier, n_row - 1 + n_col - 1)
    for side in range(2):
        @pl.when(sides[side][0])
        def _():
            y_copy(side).start()

    def first_pack(k, carry):
        fx, fz = zero, zero
        for j in range(size):
            z = k * size + j
            ex, ey, ez = e_s[0, z], e_s[1, z], e_s[2, z]
            hy, hz = h_s[1, z + 1], h_s[2, z + 1]
            up_out[k, j:j + 1, :] = ey[0:1]
            up_out[k, size + j:size + j + 1, :] = ez[0:1]
            down_out[k, j:j + 1, :] = hy[nx - 1:nx]
            down_out[k, size + j:size + j + 1, :] = hz[nx - 1:nx]
            for c, value in enumerate((ex, ey, ez)):
                last_x[c, k, j:j + 1, :] = value[nx - 1:nx]
            at = lane == j * width + width - 1
            fx = jnp.where(at, pltpu.roll(ex, j * width + width - 1, 1), fx)
            fz = jnp.where(at, pltpu.roll(ez, j * width + width - 1, 1), fz)
        first_y[0, k] = fx
        first_y[1, k] = fz
        return carry

    lax.fori_loop(0, chunks, first_pack, 0)

    for side in range(2):
        @pl.when(sides[side][0])
        def _():
            y_arrival(side).wait_recv()

    def unpack(q, carry):
        for c in range(7):
            a, b = y_in[0, c, q], y_in[1, c, q]
            values = jnp.where(on_left, a, pltpu.roll(b, half, 1)), jnp.where(on_left, pltpu.roll(a, half, 1), b)
            for i in range(2):
                if c < 3:
                    side_e[c, 2 * q + i] = values[i]
                elif c < 6:
                    side_h[c - 3, 2 * q + i + 1] = values[i]
                else:
                    side_coef[2 * q + i] = values[i]
        return carry

    lax.fori_loop(0, nz // group, unpack, 0)

    def z_after(here, after):
        return jnp.where(block == size - 1, pltpu.roll(after, half - width, 1), pltpu.roll(here, ny - width, 1))

    def z_before(here, prior):
        return jnp.where(block == 0, pltpu.roll(prior, half + width, 1), pltpu.roll(here, width, 1))

    def y_after(here, edge):
        return jnp.where(spot == width - 1, edge, pltpu.roll(here, ny - 1, 1))

    def y_before(here, edge):
        return jnp.where(spot == 0, edge, pltpu.roll(here, 1, 1))

    def spread(value):
        return jnp.broadcast_to(value, (nx, ny))

    def below(k):
        ex, ey, ez = last_x[0, k], last_x[1, k], last_x[2, k]
        hdy, hgy, ldx, lgx = prof[2], prof[3], prof[10], prof[11]
        ex_dz = jnp.where(sub == nx - 1, spread(last_x[0, k + 1, 0:1, :]), pltpu.roll(ex, nx - 1, 0)) - ex
        corner = jnp.where(lane == half + width * sub, spread(side_e[0, k, nx - 1:nx, :]), 0.0)
        corner = jnp.sum(corner, axis=1, keepdims=True)
        ex_dy = jnp.where(lane == ny - 1, corner, pltpu.roll(ex, ny - 1, 1)) - ex
        p1 = ldx * row_psi[0, k] - lgx * ez
        p2 = ldx * row_psi[1, k] - lgx * ey
        p3 = hdy * row_psi[2, k] + hgy * ex_dy
        row_psi[0, k], row_psi[1, k], row_psi[2, k] = p1, p2, p3
        down_out[k, 0:size, :] = down_out[k, 0:size, :] - time_step * (ex_dz + ez - p1)
        down_out[k, size:2 * size, :] = down_out[k, size:2 * size, :] - time_step * (p2 - ey - ex_dy - p3)
        ex, ey, ez = side_e[0, k], side_e[1, k], side_e[2, k]
        hdx, hgx, hdy, hgy = prof[0], prof[1], prof[12], prof[13]
        ex_dz = z_after(ex, side_e[0, k + 1]) - ex
        ex_dy = y_after(ex, first_y[0, k]) - ex
        p1 = hdx * side_psi[1, k] - hgx * ez
        p2 = hdx * side_psi[2, k] - hgx * ey
        p3 = hdy * side_psi[3, k] + hgy * ex_dy
        hy = side_h[1, k + 1] - side_step * (ex_dz + ez - p1)
        hz = side_h[2, k + 1] - side_step * (p2 - ey - ex_dy - p3)
        down_out[k, 2 * size:2 * size + 1, :] = hy[nx - 1:nx]
        down_out[k, 2 * size + 1:2 * size + 2, :] = hz[nx - 1:nx]

    def first_send(k, carry):
        up_out[k, 2 * size:2 * size + 1, :] = side_e[1, k, 0:1, :]
        up_out[k, 2 * size + 1:2 * size + 2, :] = side_e[2, k, 0:1, :]
        start(0, 0, k)
        below(k)
        start(1, 0, k)
        return carry

    lax.fori_loop(0, chunks, first_send, 0)
    piece = n_modes // STEPS

    def mode_copies(s):
        return [
            pltpu.make_async_remote_copy(
                src_ref=basis_in.at[pl.ds(s * piece, piece), pl.ds(pl.multiple_of(peer * nx, nx), nx)],
                dst_ref=modes_3d.at[pl.ds(row * n_modes + s * piece, piece)],
                send_sem=mode_send.at[k, s], recv_sem=mode_recv.at[k, s],
                device_id={"row": peer, "col": col}, device_id_type=pl.DeviceIdType.MESH)
            for k, peer in enumerate(row_peers)
        ]

    def tick(s, slot, k):
        more = s < STEPS - 1
        hdx, hgx, hdy, hgy = prof[0], prof[1], prof[2], prof[3]
        edx, egx, edy, egy = prof[4], prof[5], prof[6], prof[7]
        bdx, bgx = prof[8], prof[9]
        sdy, sgy = prof[12], prof[13]
        wait_recv(0, slot, k)
        ex, ey, ez = side_e[0, k], side_e[1, k], side_e[2, k]
        edge_ex, edge_ez = ex, ez
        row_y = spread(up_in[slot, k, 2 * size:2 * size + 1, :])
        row_z = spread(up_in[slot, k, 2 * size + 1:2 * size + 2, :])
        ey_dz = z_after(ey, side_e[1, k + 1]) - ey
        ex_dz = z_after(ex, side_e[0, k + 1]) - ex
        ez_dy = y_after(ez, first_y[1, k]) - ez
        ex_dy = y_after(ex, first_y[0, k]) - ex
        ez_dx = jnp.where(sub == nx - 1, row_z, pltpu.roll(ez, nx - 1, 0)) - ez
        ey_dx = jnp.where(sub == nx - 1, row_y, pltpu.roll(ey, nx - 1, 0)) - ey
        p0 = sdy * side_psi[0, k] + sgy * ez_dy
        p1 = hdx * side_psi[1, k] + hgx * ez_dx
        p2 = hdx * side_psi[2, k] + hgx * ey_dx
        p3 = sdy * side_psi[3, k] + sgy * ex_dy
        side_psi[0, k], side_psi[1, k], side_psi[2, k], side_psi[3, k] = p0, p1, p2, p3
        side_hx = side_h[0, k + 1] - side_step * (ez_dy + p0 - ey_dz)
        side_hy = side_h[1, k + 1] - side_step * (ex_dz - ez_dx - p1)
        side_hz = side_h[2, k + 1] - side_step * (ey_dx + p2 - ex_dy - p3)
        side_h[0, k + 1], side_h[1, k + 1], side_h[2, k + 1] = side_hx, side_hy, side_hz

        ey, ez = up_out[k, 0:size, :], up_out[k, size:2 * size, :]
        p1 = bdx * before_psi[0, k] + bgx * ez
        p2 = bdx * before_psi[1, k] + bgx * ey
        before_psi[0, k], before_psi[1, k] = p1, p2
        hy = before[0, k] + time_step * (ez + p1)
        hz = before[1, k] - time_step * (ey + p2)
        before[0, k], before[1, k] = hy, hz
        ey, ez = up_out[k, 2 * size:2 * size + 1, :], up_out[k, 2 * size + 1:2 * size + 2, :]
        factor = side_step[0:1] * (1.0 + bgx[0:1])
        wait_recv(1, slot, k)
        before_h[0:size, :] = up_mask * (hy + down_in[slot, k, 0:size, :])
        before_h[size:2 * size, :] = up_mask * (hz + down_in[slot, k, size:2 * size, :])
        back_y = up_mask * (down_in[slot, k, 2 * size:2 * size + 1, :] + factor * ez)
        back_z = up_mask * (down_in[slot, k, 2 * size + 1:2 * size + 2, :] - factor * ey)

        wait_send(0, slot, k)

        last_hx, last_hz, first_ex, first_ez = zero, zero, zero, zero
        below_hx, below_hy = h_s[0, k * size], h_s[1, k * size]
        ex, ey, ez = e_s[0, k * size], e_s[1, k * size], e_s[2, k * size]
        for j in range(size):
            z = k * size + j
            next_ex, next_ey, next_ez = e_s[0, z + 1], e_s[1, z + 1], e_s[2, z + 1]
            row_y = spread(up_in[slot, k, j:j + 1, :])
            row_z = spread(up_in[slot, k, size + j:size + j + 1, :])
            to_end = (ny - 1 - half - width * j) % ny
            col_x = pltpu.roll(edge_ex, to_end, 1)
            col_z = pltpu.roll(edge_ez, to_end, 1)
            ey_dz = next_ey - ey
            ex_dz = next_ex - ex
            ez_dy = jnp.where(lane == ny - 1, col_z, pltpu.roll(ez, ny - 1, 1)) - ez
            ex_dy = jnp.where(lane == ny - 1, col_x, pltpu.roll(ex, ny - 1, 1)) - ex
            ez_dx = jnp.where(sub == nx - 1, row_z, pltpu.roll(ez, nx - 1, 0)) - ez
            ey_dx = jnp.where(sub == nx - 1, row_y, pltpu.roll(ey, nx - 1, 0)) - ey
            p0 = hdy * psi[0, z] + hgy * ez_dy
            p1 = hdx * psi[1, z] + hgx * ez_dx
            p2 = hdx * psi[2, z] + hgx * ey_dx
            p3 = hdy * psi[3, z] + hgy * ex_dy
            psi[0, z], psi[1, z], psi[2, z], psi[3, z] = p0, p1, p2, p3
            hx = h_s[0, z + 1] - time_step * (ez_dy + p0 - ey_dz)
            hy = h_s[1, z + 1] - time_step * (ex_dz - ez_dx - p1)
            hz = h_s[2, z + 1] - time_step * (ey_dx + p2 - ex_dy - p3)
            h_s[0, z + 1], h_s[1, z + 1], h_s[2, z + 1] = hx, hy, hz
            at = lane == half + width * j
            last_hx = jnp.where(at, pltpu.roll(hx, (half + width * j + 1) % ny, 1), last_hx)
            last_hz = jnp.where(at, pltpu.roll(hz, (half + width * j + 1) % ny, 1), last_hz)

            row_y = spread(before_h[j:j + 1, :])
            row_z = spread(before_h[size + j:size + j + 1, :])
            to_start = ny - (width * j + width - 1)
            col_x = pltpu.roll(side_hx, to_start, 1)
            col_z = pltpu.roll(side_hz, to_start, 1)
            hy_dz = hy - below_hy
            hx_dz = hx - below_hx
            hz_dy = hz - jnp.where(lane == 0, col_z, pltpu.roll(hz, 1, 1))
            hx_dy = hx - jnp.where(lane == 0, col_x, pltpu.roll(hx, 1, 1))
            hz_dx = hz - jnp.where(sub == 0, row_z, pltpu.roll(hz, 1, 0))
            hy_dx = hy - jnp.where(sub == 0, row_y, pltpu.roll(hy, 1, 0))
            p0 = edy * psi[4, z] + egy * hz_dy
            p1 = edx * psi[5, z] + egx * hz_dx
            p2 = edx * psi[6, z] + egx * hy_dx
            p3 = edy * psi[7, z] + egy * hx_dy
            psi[4, z], psi[5, z], psi[6, z], psi[7, z] = p0, p1, p2, p3
            amount = coef_s[z]
            ex = ex + amount * (hz_dy + p0 - hy_dz)
            ey = ey + amount * (hx_dz - hz_dx - p1)
            ez = ez + amount * (hy_dx + p2 - hx_dy - p3)
            e_s[0, z], e_s[1, z], e_s[2, z] = ex, ey, ez
            at = lane == width * j + width - 1
            first_ex = jnp.where(at, pltpu.roll(ex, width * j + width - 1, 1), first_ex)
            first_ez = jnp.where(at, pltpu.roll(ez, width * j + width - 1, 1), first_ez)
            up_out[k, j:j + 1, :] = ey[0:1]
            up_out[k, size + j:size + j + 1, :] = ez[0:1]
            for c, value in enumerate((ex, ey, ez)):
                last_x[c, k, j:j + 1, :] = value[nx - 1:nx]
            below_hx, below_hy = hx, hy
            ex, ey, ez = next_ex, next_ey, next_ez
        first_y[0, k] = first_ex
        first_y[1, k] = first_ez

        sdy, sgy = prof[14], prof[15]
        hx, hy, hz = side_hx, side_hy, side_hz
        hy_dz = hy - z_before(hy, side_h[1, k])
        hx_dz = hx - z_before(hx, side_h[0, k])
        hz_dy = hz - y_before(hz, last_hz)
        hx_dy = hx - y_before(hx, last_hx)
        hz_dx = hz - jnp.where(sub == 0, spread(back_z), pltpu.roll(hz, 1, 0))
        hy_dx = hy - jnp.where(sub == 0, spread(back_y), pltpu.roll(hy, 1, 0))
        p0 = sdy * side_psi[4, k] + sgy * hz_dy
        p1 = edx * side_psi[5, k] + egx * hz_dx
        p2 = edx * side_psi[6, k] + egx * hy_dx
        p3 = sdy * side_psi[7, k] + sgy * hx_dy
        side_psi[4, k], side_psi[5, k], side_psi[6, k], side_psi[7, k] = p0, p1, p2, p3
        amount = side_coef[k]
        ex = side_e[0, k] + amount * (hz_dy + p0 - hy_dz)
        ey = side_e[1, k] + amount * (hx_dz - hz_dx - p1)
        ez = side_e[2, k] + amount * (hy_dx + p2 - hx_dy - p3)
        side_e[0, k], side_e[1, k], side_e[2, k] = ex, ey, ez
        up_out[k, 2 * size:2 * size + 1, :] = ey[0:1]
        up_out[k, 2 * size + 1:2 * size + 2, :] = ez[0:1]

        @pl.when(more)
        def _():
            start(0, 1 - slot, k)

    def send_below(s, slot, k):
        wait_send(1, slot, k)

        @pl.when(s < STEPS - 1)
        def _():
            below(k)
            start(1, 1 - slot, k)

    def step(s, carry):
        slot = lax.rem(s, 2)
        for copy in mode_copies(s):
            copy.start()

        def body(k, carry):
            tick(s, slot, k)

            @pl.when(k > 0)
            def _():
                send_below(s, slot, k - 1)

            return carry

        lax.fori_loop(0, chunks, body, 0)
        send_below(s, slot, chunks - 1)
        return carry

    lax.fori_loop(0, STEPS, step, 0)
    for side in range(2):
        @pl.when(sides[side][0])
        def _():
            y_copy(side).wait_send()

    store_e = pltpu.make_async_copy(e_s.at[:, pl.ds(0, nz)], e_out, local_sem.at[0])
    store_h = pltpu.make_async_copy(h_s.at[:, pl.ds(1, nz)], h_out, local_sem.at[1])
    store_e.start()
    store_h.start()

    count = snaps.shape[0] // nx

    def pick(s, carry):
        planes = []
        for j in range(8):
            index = index_ref[s * 8 + j]
            c = index // nz
            planes.append(fields[c, index - c * nz + (c // 3)])
        for j in range(8):
            snaps[pl.ds(pl.multiple_of((s * 8 + j) * nx, nx), nx), :] = planes[j]
        return carry

    lax.fori_loop(0, count // 8, pick, 0)
    load_b.wait()

    def wait_modes(s, carry):
        for copy in mode_copies(s):
            copy.wait()
        return carry

    lax.fori_loop(0, STEPS, wait_modes, 0)
    n_all = modes.shape[0] // nx
    dims = (((1,), (1,)), ((), ()))
    proj, gram = None, None
    for x in range(nx):
        a = snaps[pl.ds(x, count, stride=nx), :]
        b = modes[pl.ds(x, n_all, stride=nx), :]
        p = lax.dot_general(a, b, dims, precision=lax.Precision.HIGHEST, preferred_element_type=jnp.float32)
        g = lax.dot_general(a, a, dims, precision=lax.Precision.HIGHEST, preferred_element_type=jnp.float32)
        proj, gram = (p, g) if x == 0 else (proj + p, gram + g)
    part[:, 0:n_all] = proj
    part[:, n_all:n_all + count] = gram / float(nx * n_row * ny * n_col)

    share = count // n_row
    own = pl.ds(pl.multiple_of(row * share, share), share)

    def exchange(peers, axis, src_of, dst, sends, recvs):
        result = []
        for k, peer in enumerate(peers):
            where = {"row": row, "col": col}
            where[axis] = peer
            result.append(pltpu.make_async_remote_copy(
                src_ref=src_of(peer), dst_ref=dst, send_sem=sends.at[k], recv_sem=recvs.at[k],
                device_id=where, device_id_type=pl.DeviceIdType.MESH))
        for copy in result:
            copy.start()
        for copy in result:
            copy.wait()

    row_sums[row] = part[own, :]
    exchange(
        row_peers, "row", lambda peer: part.at[pl.ds(pl.multiple_of(peer * share, share), share)],
        row_sums.at[row], sum_send, sum_recv)
    value = row_sums[0]
    for k in range(1, n_row):
        value = value + row_sums[k]
    col_sums[col] = value
    exchange(col_peers, "col", lambda peer: col_sums.at[col], col_sums.at[col], col_send, col_recv)
    value = col_sums[0]
    for k in range(1, n_col):
        value = value + col_sums[k]
    total[own, :] = value
    exchange(row_peers, "row", lambda peer: total.at[own], total.at[own], back_send, back_recv)
    proj_out[...] = total[:, 0:n_all]
    gram_out[...] = total[:, n_all:n_all + count]
    store_e.wait()
    store_h.wait()


def shards(e_field, h_field, e_coef, basis, pml_width, snap_index):
    nz, nx, ny = e_coef.shape
    n_row, n_col = lax.axis_size("row"), lax.axis_size("col")
    modes, count = basis.shape[0] * n_row, snap_index.shape[0]
    f32 = jnp.float32
    size = ny // STEPS // 2
    chunks = nz // size
    wide = modes + (count + 127) // 128 * 128
    any_space = pl.BlockSpec(memory_space=pl.ANY)
    smem, vmem = pl.BlockSpec(memory_space=pltpu.SMEM), pl.BlockSpec(memory_space=pltpu.VMEM)
    return pl.pallas_call(
        functools.partial(step_kernel, n_row, n_col),
        out_shape=[
            jax.ShapeDtypeStruct(e_field.shape, f32), jax.ShapeDtypeStruct(h_field.shape, f32),
            jax.ShapeDtypeStruct((count, modes), f32), jax.ShapeDtypeStruct((count, count), f32),
        ],
        in_specs=[smem, smem, any_space, any_space, any_space, any_space],
        out_specs=[any_space, any_space, vmem, vmem],
        scratch_shapes=[
            pltpu.VMEM((6, nz + 1, nx, ny), f32),
            pltpu.VMEM((nz, nx, ny), f32), pltpu.VMEM((8, nz, nx, ny), f32),
            pltpu.VMEM((3, chunks + 1, nx, ny), f32), pltpu.VMEM((3, chunks + 1, nx, ny), f32),
            pltpu.VMEM((chunks, nx, ny), f32), pltpu.VMEM((8, chunks, nx, ny), f32),
            pltpu.VMEM((2, chunks, nx, ny), f32),
            pltpu.VMEM((2, 7, chunks // 2, nx, ny), f32), pltpu.VMEM((2, 7, chunks // 2, nx, ny), f32),
            pltpu.VMEM((chunks, 3 * size, ny), f32), pltpu.VMEM((2, chunks, 3 * size, ny), f32),
            pltpu.VMEM((chunks, 3 * size, ny), f32), pltpu.VMEM((2, chunks, 3 * size, ny), f32),
            pltpu.VMEM((3, chunks + 1, size, ny), f32), pltpu.VMEM((3, chunks, size, ny), f32),
            pltpu.VMEM((2, chunks, size, ny), f32), pltpu.VMEM((2, chunks, size, ny), f32),
            pltpu.VMEM((2 * size, ny), f32),
            pltpu.VMEM((16, nx, ny), f32),
            pltpu.VMEM((modes * nx, ny), f32), pltpu.VMEM((count * nx, ny), f32),
            pltpu.VMEM((count, wide), f32), pltpu.VMEM((n_row, count // n_row, wide), f32),
            pltpu.VMEM((n_col, count // n_row, wide), f32), pltpu.VMEM((count, wide), f32),
            pltpu.SemaphoreType.DMA((4,)),
            pltpu.SemaphoreType.DMA((2,)), pltpu.SemaphoreType.DMA((2,)),
            pltpu.SemaphoreType.DMA((2, 2, chunks)), pltpu.SemaphoreType.DMA((2, 2, chunks)),
            pltpu.SemaphoreType.DMA((n_row - 1, STEPS)), pltpu.SemaphoreType.DMA((n_row - 1, STEPS)),
            pltpu.SemaphoreType.DMA((n_row - 1,)), pltpu.SemaphoreType.DMA((n_row - 1,)),
            pltpu.SemaphoreType.DMA((n_col - 1,)), pltpu.SemaphoreType.DMA((n_col - 1,)),
            pltpu.SemaphoreType.DMA((n_row - 1,)), pltpu.SemaphoreType.DMA((n_row - 1,)),
        ],
        compiler_params=pltpu.CompilerParams(
            collective_id=0, has_side_effects=True, vmem_limit_bytes=67_043_328
        ),
    )(pml_width, snap_index, e_field, h_field, e_coef, basis)


def solution(mesh):
    in_specs = (
        P(None, None, "row", "col"),
        P(None, None, "row", "col"),
        P(None, "row", "col"),
        P("row", None, "col"),
        P(),
        P(),
    )
    out_specs = (P(None, None, "row", "col"), P(None, None, "row", "col"), P(), P())
    return jax.shard_map(shards, mesh=mesh, in_specs=in_specs, out_specs=out_specs, check_vma=False)
```

time: 76.9 us -> 63.8 us (0.83)
  Pallas kernels: 71.6 us -> 58.5 us
    pallas_call x1, Pallas kernels: 71.6 us -> 58.5 us  [shards(): pl.pallas_call(functools.partial(step_kernel, n_row, n_col), out_shape=[j...]
where the time goes in v1:
time: 63.8 us; the launch traced here: 63.5 us
  Pallas kernels  58.5 us (92%)
  local copies, waits for them, and re-layouts  4.41 us (7%)
  between operations  0.65 us (1%)
    pallas_call x1, Pallas kernels, shards(): pl.pallas_call(functools.partial(step_kernel, n_row, n_col), out_shape=[j...  58.5 us
    unnamed x10, local copies, waits for them, and re-layouts  4.41 us

profile of v1, /device:TPU:0, one launch (start us, length us, event | category | flops | bytes accessed | tf_op | source)
XLA Modules:
  0.0 63.5 jit_solution(1111514987494403275)
XLA Ops:
  0.6 58.5 %shard_map.93 = (f32[3,64,8,128]{3,2,1,0:T(8,128)}, f32[3,64,8,128]{3,2,1,0:T(8,128)}, f32[64,128]{1,0:T(8,128)}, f32[64,64]{1,0:T(8,128)}) custom-call(s32[4]{0:T(128)} %width_ref.1, s32[64]{0:T(128)} %index_ref.1, f32[3,64,8,128]{3,2,1,0:T(8,128)} %e_in.1, f32[3,64,8,128]{3,2,1,0:T(8,128)} %h_in.1, f32[64,8,128]{2,1,0:T(8,128)} %coef_in.1, ...), custom_call_target="tpu_custom_call" | custom-call | tf_op jit(solution)/shard_map/pallas_call | solution.py:533
  59.1 0.0 copy-start
  59.1 2.1 %copy.14 = f32[3,64,8,128]{3,2,1,0:T(8,128)} copy(f32[3,64,8,128]{3,2,1,0:T(8,128)} %get-tuple-element.8) | data formatting | bytes 1572864
  61.3 0.0 copy-done
  61.3 0.0 copy-start.2
  61.3 0.9 %copy.15 = f32[3,64,8,128]{3,2,1,0:T(8,128)} copy(f32[3,64,8,128]{3,2,1,0:T(8,128)S(1)} %copy-done) | data formatting | bytes 1572864
  62.2 0.0 copy-done.2
  62.2 0.0 copy-start.1
  62.2 0.6 copy.16
  62.8 0.2 copy-done.1
  62.9 0.6 copy.17
Async XLA Ops:
  59.1 2.1 %copy-start = (f32[3,64,8,128]{3,2,1,0:T(8,128)S(1)}, f32[3,64,8,128]{3,2,1,0:T(8,128)}, u32[]{:S(2)}) copy-start(f32[3,64,8,128]{3,2,1,0:T(8,128)} %get-tuple-element.9) | copy-start | bytes 2359300
  61.3 0.9 %copy-start.2 = (f32[64,128]{1,0:T(8,128)S(1)}, f32[64,128]{1,0:T(8,128)}, u32[]{:S(2)}) copy-start(f32[64,128]{1,0:T(8,128)} %get-tuple-element.10) | copy-start | bytes 98308
  62.2 0.8 %copy-start.1 = (f32[64,64]{1,0:T(8,128)S(1)}, f32[64,64]{1,0:T(8,128)}, u32[]{:S(2)}) copy-start(f32[64,64]{1,0:T(8,128)} %get-tuple-element.11) | copy-start | bytes 49156

commit v2 on v1

--- a/solution.py
+++ b/solution.py
@@ -24,14 +24,13 @@
 
 
 def step_kernel(
-    n_row, n_col, width_ref, index_ref, e_in, h_in, coef_in, basis_in, e_out, h_out, proj_out, gram_out,
-    fields, coef_s, psi, side_e, side_h, side_coef, side_psi, first_y, y_out, y_in,
+    n_row, n_col, width_ref, index_ref, e_in, h_in, coef_in, basis_in, e_s, h_s, total,
+    coef_s, psi, side_e, side_h, side_coef, side_psi, first_y, y_out, y_in,
     up_out, up_in, down_out, down_in, last_x, row_psi, before, before_psi, before_h,
-    prof, modes, snaps, part, row_sums, col_sums, total,
+    prof, modes, snaps, part, row_sums, col_sums,
     local_sem, y_send, y_recv, x_send, x_recv, mode_send, mode_recv,
     sum_send, sum_recv, col_send, col_recv, back_send, back_recv,
 ):
-    e_s, h_s = fields.at[pl.ds(0, 3)], fields.at[pl.ds(3, 3)]
     nz, nx, ny = coef_s.shape
     width = STEPS
     group = ny // width
@@ -55,8 +54,13 @@
         modes_3d.at[pl.ds(row * n_modes, n_modes)], local_sem.at[3])
     load_b.start()
     row_peers = [lax.rem(row + k, n_row) for k in range(1, n_row)]
-    col_peers = [lax.rem(col + k, n_col) for k in range(1, n_col)]
-
+    pair = lax.rem(col, 2)
+    near = [
+        {"row": lax.rem(row + k, n_row), "col": col - pair + lax.rem(pair + m, 2)}
+        for k in range(n_row) for m in range(2) if k + m]
+    far = [{"row": row, "col": lax.rem(col + 2 * k, n_col)} for k in range(1, n_col // 2)]
+    other = col - 1 + 2 * pair
+    beside = jnp.logical_and(other >= 0, other < n_col)
     part[...] = jnp.zeros_like(part)
     up_in[...] = jnp.zeros_like(up_in)
     down_in[...] = jnp.zeros_like(down_in)
@@ -66,12 +70,13 @@
             y_in[side] = jnp.zeros(y_in.shape[1:], jnp.float32)
 
     barrier = pltpu.get_barrier_semaphore()
-    for peer in row_peers:
+    for peer in near + far:
+        pl.semaphore_signal(barrier, inc=1, device_id=peer, device_id_type=pl.DeviceIdType.MESH)
+
+    @pl.when(beside)
+    def _():
         pl.semaphore_signal(
-            barrier, inc=1, device_id={"row": peer, "col": col}, device_id_type=pl.DeviceIdType.MESH)
-    for peer in col_peers:
-        pl.semaphore_signal(
-            barrier, inc=1, device_id={"row": row, "col": peer}, device_id_type=pl.DeviceIdType.MESH)
+            barrier, inc=1, device_id={"row": row, "col": other}, device_id_type=pl.DeviceIdType.MESH)
 
     zero = jnp.zeros((nx, ny), jnp.float32)
     for c in range(3):
@@ -174,7 +179,7 @@
         return carry
 
     lax.fori_loop(0, nz // group, pack_sides, 0)
-    pl.semaphore_wait(barrier, n_row - 1 + n_col - 1)
+    pl.semaphore_wait(barrier, len(near) + len(far) + beside.astype(jnp.int32))
     for side in range(2):
         @pl.when(sides[side][0])
         def _():
@@ -446,11 +451,6 @@
         def _():
             y_copy(side).wait_send()
 
-    store_e = pltpu.make_async_copy(e_s.at[:, pl.ds(0, nz)], e_out, local_sem.at[0])
-    store_h = pltpu.make_async_copy(h_s.at[:, pl.ds(1, nz)], h_out, local_sem.at[1])
-    store_e.start()
-    store_h.start()
-
     count = snaps.shape[0] // nx
 
     def pick(s, carry):
@@ -458,7 +458,10 @@
         for j in range(8):
             index = index_ref[s * 8 + j]
             c = index // nz
-            planes.append(fields[c, index - c * nz + (c // 3)])
+            z = index - c * nz
+            e_plane = e_s[jnp.minimum(c, 2), z]
+            h_plane = h_s[jnp.maximum(c - 3, 0), z + 1]
+            planes.append(jnp.where(c < 3, e_plane, h_plane))
         for j in range(8):
             snaps[pl.ds(pl.multiple_of((s * 8 + j) * nx, nx), nx), :] = planes[j]
         return carry
@@ -481,41 +484,52 @@
         p = lax.dot_general(a, b, dims, precision=lax.Precision.HIGHEST, preferred_element_type=jnp.float32)
         g = lax.dot_general(a, a, dims, precision=lax.Precision.HIGHEST, preferred_element_type=jnp.float32)
         proj, gram = (p, g) if x == 0 else (proj + p, gram + g)
-    part[:, 0:n_all] = proj
-    part[:, n_all:n_all + count] = gram / float(nx * n_row * ny * n_col)
-
-    share = count // n_row
-    own = pl.ds(pl.multiple_of(row * share, share), share)
-
-    def exchange(peers, axis, src_of, dst, sends, recvs):
+    gram = gram / float(nx * n_row * ny * n_col)
+    share = part.shape[1]
+    for k in range(part.shape[0]):
+        part[k, :, 0:n_all] = proj[k * share:(k + 1) * share]
+        part[k, :, n_all:n_all + count] = gram[k * share:(k + 1) * share]
+    own = 2 * row + pair
+
+    def exchange(peers, src_of, dst, sends, recvs):
         result = []
         for k, peer in enumerate(peers):
-            where = {"row": row, "col": col}
-            where[axis] = peer
             result.append(pltpu.make_async_remote_copy(
                 src_ref=src_of(peer), dst_ref=dst, send_sem=sends.at[k], recv_sem=recvs.at[k],
-                device_id=where, device_id_type=pl.DeviceIdType.MESH))
+                device_id=peer, device_id_type=pl.DeviceIdType.MESH))
         for copy in result:
             copy.start()
         for copy in result:
             copy.wait()
 
-    row_sums[row] = part[own, :]
+    row_sums[own] = part[own]
     exchange(
-        row_peers, "row", lambda peer: part.at[pl.ds(pl.multiple_of(peer * share, share), share)],
-        row_sums.at[row], sum_send, sum_recv)
+        near, lambda peer: part.at[2 * peer["row"] + lax.rem(peer["col"], 2)],
+        row_sums.at[own], sum_send, sum_recv)
     value = row_sums[0]
-    for k in range(1, n_row):
+    for k in range(1, 2 * n_row):
         value = value + row_sums[k]
-    col_sums[col] = value
-    exchange(col_peers, "col", lambda peer: col_sums.at[col], col_sums.at[col], col_send, col_recv)
+    level = lax.div(col, 2)
+    col_sums[level] = value
+    exchange(far, lambda peer: col_sums.at[level], col_sums.at[level], col_send, col_recv)
     value = col_sums[0]
-    for k in range(1, n_col):
+    for k in range(1, n_col // 2):
         value = value + col_sums[k]
-    total[own, :] = value
-    exchange(row_peers, "row", lambda peer: total.at[own], total.at[own], back_send, back_recv)
-    proj_out[...] = total[:, 0:n_all]
-    gram_out[...] = total[:, n_all:n_all + count]
+    total[own] = value
+    exchange(near, lambda peer: total.at[own], total.at[own], back_send, back_recv)
+
+
+def write_kernel(e_s, h_s, total, e_out, h_out, proj_out, gram_out, sems):
+    nz = e_out.shape[1]
+    store_e = pltpu.make_async_copy(e_s.at[:, pl.ds(0, nz)], e_out, sems.at[0])
+    store_h = pltpu.make_async_copy(h_s.at[:, pl.ds(1, nz)], h_out, sems.at[1])
+    store_e.start()
+    store_h.start()
+    n_all, count = proj_out.shape[1], gram_out.shape[1]
+    share = total.shape[1]
+    for k in range(total.shape[0]):
+        proj_out[k * share:(k + 1) * share, :] = total[k, :, 0:n_all]
+        gram_out[k * share:(k + 1) * share, :] = total[k, :, n_all:n_all + count]
     store_e.wait()
     store_h.wait()
 
@@ -528,18 +542,16 @@
     size = ny // STEPS // 2
     chunks = nz // size
     wide = modes + (count + 127) // 128 * 128
-    any_space = pl.BlockSpec(memory_space=pl.ANY)
+    any_space = pl.BlockSpec(memory_space=pltpu.HBM)
     smem, vmem = pl.BlockSpec(memory_space=pltpu.SMEM), pl.BlockSpec(memory_space=pltpu.VMEM)
-    return pl.pallas_call(
+    held = pltpu.VMEM((3, nz + 1, nx, ny), f32)
+    share = count // (2 * n_row)
+    e_s, h_s, total = pl.pallas_call(
         functools.partial(step_kernel, n_row, n_col),
-        out_shape=[
-            jax.ShapeDtypeStruct(e_field.shape, f32), jax.ShapeDtypeStruct(h_field.shape, f32),
-            jax.ShapeDtypeStruct((count, modes), f32), jax.ShapeDtypeStruct((count, count), f32),
-        ],
+        out_shape=[held, held, pltpu.VMEM((2 * n_row, share, wide), f32)],
         in_specs=[smem, smem, any_space, any_space, any_space, any_space],
-        out_specs=[any_space, any_space, vmem, vmem],
+        out_specs=[vmem, vmem, vmem],
         scratch_shapes=[
-            pltpu.VMEM((6, nz + 1, nx, ny), f32),
             pltpu.VMEM((nz, nx, ny), f32), pltpu.VMEM((8, nz, nx, ny), f32),
             pltpu.VMEM((3, chunks + 1, nx, ny), f32), pltpu.VMEM((3, chunks + 1, nx, ny), f32),
             pltpu.VMEM((chunks, nx, ny), f32), pltpu.VMEM((8, chunks, nx, ny), f32),
@@ -552,20 +564,31 @@
             pltpu.VMEM((2 * size, ny), f32),
             pltpu.VMEM((16, nx, ny), f32),
             pltpu.VMEM((modes * nx, ny), f32), pltpu.VMEM((count * nx, ny), f32),
-            pltpu.VMEM((count, wide), f32), pltpu.VMEM((n_row, count // n_row, wide), f32),
-            pltpu.VMEM((n_col, count // n_row, wide), f32), pltpu.VMEM((count, wide), f32),
+            pltpu.VMEM((2 * n_row, share, wide), f32), pltpu.VMEM((2 * n_row, share, wide), f32),
+            pltpu.VMEM((n_col // 2, share, wide), f32),
             pltpu.SemaphoreType.DMA((4,)),
             pltpu.SemaphoreType.DMA((2,)), pltpu.SemaphoreType.DMA((2,)),
             pltpu.SemaphoreType.DMA((2, 2, chunks)), pltpu.SemaphoreType.DMA((2, 2, chunks)),
             pltpu.SemaphoreType.DMA((n_row - 1, STEPS)), pltpu.SemaphoreType.DMA((n_row - 1, STEPS)),
-            pltpu.SemaphoreType.DMA((n_row - 1,)), pltpu.SemaphoreType.DMA((n_row - 1,)),
-            pltpu.SemaphoreType.DMA((n_col - 1,)), pltpu.SemaphoreType.DMA((n_col - 1,)),
-            pltpu.SemaphoreType.DMA((n_row - 1,)), pltpu.SemaphoreType.DMA((n_row - 1,)),
+            pltpu.SemaphoreType.DMA((2 * n_row - 1,)), pltpu.SemaphoreType.DMA((2 * n_row - 1,)),
+            pltpu.SemaphoreType.DMA((n_col // 2 - 1,)), pltpu.SemaphoreType.DMA((n_col // 2 - 1,)),
+            pltpu.SemaphoreType.DMA((2 * n_row - 1,)), pltpu.SemaphoreType.DMA((2 * n_row - 1,)),
         ],
         compiler_params=pltpu.CompilerParams(
-            collective_id=0, has_side_effects=True, vmem_limit_bytes=67_043_328
+            collective_id=0, has_side_effects=True, vmem_limit_bytes=65_280_000
         ),
     )(pml_width, snap_index, e_field, h_field, e_coef, basis)
+    return pl.pallas_call(
+        write_kernel,
+        out_shape=[
+            jax.ShapeDtypeStruct(e_field.shape, f32), jax.ShapeDtypeStruct(h_field.shape, f32),
+            jax.ShapeDtypeStruct((count, modes), f32), jax.ShapeDtypeStruct((count, count), f32),
+        ],
+        in_specs=[vmem, vmem, vmem],
+        out_specs=[any_space, any_space, vmem, vmem],
+        scratch_shapes=[pltpu.SemaphoreType.DMA((2,))],
+        compiler_params=pltpu.CompilerParams(vmem_limit_bytes=16_777_216),
+    )(e_s, h_s, total)
 
 
 def solution(mesh):

time: 63.8 us -> 60 us (0.940)
  local copies, waits for them, and re-layouts: 4.41 us -> 0 us
  Pallas kernels: 58.5 us -> 59.2 us
    unnamed x10 -> x0, local copies, waits for them, and re-layouts: 4.41 us -> none
    pallas_call x1 -> x2, Pallas kernels: 58.5 us -> 59.2 us  [the longest x1 57.4 us: shards(): pl.pallas_call(functools.partial(step_kernel, n_row, n_col), out_shape=[h...]
where the time goes in v2:
time: 60 us; the launch traced here: 59.8 us
  Pallas kernels  59.2 us (99%)
  between operations  0.64 us (1%)
    pallas_call x1, Pallas kernels, shards(): pl.pallas_call(functools.partial(step_kernel, n_row, n_col), out_shape=[h...  57.4 us
    pallas_call x1, Pallas kernels, shards(): pl.pallas_call(write_kernel, out_shape=[jax.ShapeDtypeStruct(e_field.shap...  1.78 us

profile of v2, /device:TPU:0, one launch (start us, length us, event | category | flops | bytes accessed | tf_op | source)
XLA Modules:
  0.0 59.8 jit_solution(8149640443189355865)
XLA Ops:
  0.6 57.4 %shard_map.93 = (f32[3,65,8,128]{3,2,1,0:T(8,128)S(1)}, f32[3,65,8,128]{3,2,1,0:T(8,128)S(1)}, f32[8,8,256]{2,1,0:T(8,128)S(1)}) custom-call(s32[4]{0:T(128)} %width_ref.1, s32[64]{0:T(128)} %index_ref.1, f32[3,64,8,128]{3,2,1,0:T(8,128)} %e_in.1, f32[3,64,8,128]{3,2,1,0:T(8,128)} %h_in.1, f32[64,8,128]{2,1,0:T(8,128)} %coef_in.1, f32[32,32,128]{2,1,0:T(8,128)} %basis_in.1), custom_call_target="tpu_custom_call" | custom-call | tf_op jit(solution)/shard_map/pallas_call | solution.py:549
  58.0 1.8 %shard_map.94 = (f32[3,64,8,128]{3,2,1,0:T(8,128)}, f32[3,64,8,128]{3,2,1,0:T(8,128)}, f32[64,128]{1,0:T(8,128)}, f32[64,64]{1,0:T(8,128)}) custom-call(f32[3,65,8,128]{3,2,1,0:T(8,128)S(1)} %get-tuple-element.7.e_s, f32[3,65,8,128]{3,2,1,0:T(8,128)S(1)} %get-tuple-element.8.h_s, f32[8,8,256]{2,1,0:T(8,128)S(1)} %get-tuple-element.9.total), custom_call_target="tpu_custom_call" | custom-call | tf_op jit(solution)/shard_map/pallas_call | solution.py:581

commit v3 on v2

--- a/solution.py
+++ b/solution.py
@@ -7,6 +7,7 @@
 from jax.sharding import PartitionSpec as P
 
 STEPS = 8
+
 
 time_step = 0.5
 sigma_top = 4.0
@@ -82,9 +83,14 @@
     for c in range(3):
         e_s[c, nz] = zero
         h_s[c, 0] = zero
-        side_e[c, chunks] = zero
         side_h[c, 0] = zero
-    last_x[0, chunks] = zero
+        side_h[c, chunks + 1] = zero
+        for k in range(2):
+            side_e[c, chunks + k] = zero
+            last_x[c, chunks + k] = zero
+    for c in range(2):
+        first_y[c, chunks] = zero
+    down_out[chunks] = jnp.zeros(down_out.shape[1:], jnp.float32)
 
     def clear(z, carry):
         for k in range(8):
@@ -149,15 +155,18 @@
 
     sides = ((left, {"row": row, "col": col - 1}), (right, {"row": row, "col": col + 1}))
 
-    def y_copy(side):
+    def y_copy(side, arriving, part):
+        parts = (pl.ds(0, 6), pl.ds(6, 1))[part]
+        a = 1 - side if arriving else side
         return pltpu.make_async_remote_copy(
-            src_ref=y_out.at[side], dst_ref=y_in.at[1 - side], send_sem=y_send.at[side],
-            recv_sem=y_recv.at[1 - side], device_id=sides[side][1], device_id_type=pl.DeviceIdType.MESH)
-
-    def y_arrival(side):
-        return pltpu.make_async_remote_copy(
-            src_ref=y_out.at[1 - side], dst_ref=y_in.at[side], send_sem=y_send.at[1 - side],
-            recv_sem=y_recv.at[side], device_id=sides[side][1], device_id_type=pl.DeviceIdType.MESH)
+            src_ref=y_out.at[a, parts], dst_ref=y_in.at[1 - a, parts], send_sem=y_send.at[a, part],
+            recv_sem=y_recv.at[1 - a, part], device_id=sides[side][1], device_id_type=pl.DeviceIdType.MESH)
+
+    def y_wait(part):
+        for side in range(2):
+            @pl.when(sides[side][0])
+            def _():
+                y_copy(side, True, part).wait_recv()
 
     load_e.wait()
     load_h.wait()
@@ -183,7 +192,8 @@
     for side in range(2):
         @pl.when(sides[side][0])
         def _():
-            y_copy(side).start()
+            for part_no in range(2):
+                y_copy(side, False, part_no).start()
 
     def first_pack(k, carry):
         fx, fz = zero, zero
@@ -206,13 +216,10 @@
 
     lax.fori_loop(0, chunks, first_pack, 0)
 
-    for side in range(2):
-        @pl.when(sides[side][0])
-        def _():
-            y_arrival(side).wait_recv()
-
-    def unpack(q, carry):
-        for c in range(7):
+    y_wait(0)
+
+    def unpack(comps, q, carry):
+        for c in comps:
             a, b = y_in[0, c, q], y_in[1, c, q]
             values = jnp.where(on_left, a, pltpu.roll(b, half, 1)), jnp.where(on_left, pltpu.roll(a, half, 1), b)
             for i in range(2):
@@ -224,7 +231,7 @@
                     side_coef[2 * q + i] = values[i]
         return carry
 
-    lax.fori_loop(0, nz // group, unpack, 0)
+    lax.fori_loop(0, nz // group, functools.partial(unpack, range(6)), 0)
 
     def z_after(here, after):
         return jnp.where(block == size - 1, pltpu.roll(after, half - width, 1), pltpu.roll(here, ny - width, 1))
@@ -241,7 +248,7 @@
     def spread(value):
         return jnp.broadcast_to(value, (nx, ny))
 
-    def below(k):
+    def below_main(k):
         ex, ey, ez = last_x[0, k], last_x[1, k], last_x[2, k]
         hdy, hgy, ldx, lgx = prof[2], prof[3], prof[10], prof[11]
         ex_dz = jnp.where(sub == nx - 1, spread(last_x[0, k + 1, 0:1, :]), pltpu.roll(ex, nx - 1, 0)) - ex
@@ -254,6 +261,7 @@
         row_psi[0, k], row_psi[1, k], row_psi[2, k] = p1, p2, p3
         down_out[k, 0:size, :] = down_out[k, 0:size, :] - time_step * (ex_dz + ez - p1)
         down_out[k, size:2 * size, :] = down_out[k, size:2 * size, :] - time_step * (p2 - ey - ex_dy - p3)
+    def below_side(k):
         ex, ey, ez = side_e[0, k], side_e[1, k], side_e[2, k]
         hdx, hgx, hdy, hgy = prof[0], prof[1], prof[12], prof[13]
         ex_dz = z_after(ex, side_e[0, k + 1]) - ex
@@ -270,11 +278,14 @@
         up_out[k, 2 * size:2 * size + 1, :] = side_e[1, k, 0:1, :]
         up_out[k, 2 * size + 1:2 * size + 2, :] = side_e[2, k, 0:1, :]
         start(0, 0, k)
-        below(k)
+        below_main(k)
+        below_side(k)
         start(1, 0, k)
         return carry
 
     lax.fori_loop(0, chunks, first_send, 0)
+    y_wait(1)
+    lax.fori_loop(0, nz // group, functools.partial(unpack, range(6, 7)), 0)
     piece = n_modes // STEPS
 
     def mode_copies(s):
@@ -287,15 +298,10 @@
             for k, peer in enumerate(row_peers)
         ]
 
-    def tick(s, slot, k):
-        more = s < STEPS - 1
-        hdx, hgx, hdy, hgy = prof[0], prof[1], prof[2], prof[3]
-        edx, egx, edy, egy = prof[4], prof[5], prof[6], prof[7]
-        bdx, bgx = prof[8], prof[9]
+    def side_magnetic(slot, k):
+        hdx, hgx = prof[0], prof[1]
         sdy, sgy = prof[12], prof[13]
-        wait_recv(0, slot, k)
         ex, ey, ez = side_e[0, k], side_e[1, k], side_e[2, k]
-        edge_ex, edge_ez = ex, ez
         row_y = spread(up_in[slot, k, 2 * size:2 * size + 1, :])
         row_z = spread(up_in[slot, k, 2 * size + 1:2 * size + 2, :])
         ey_dz = z_after(ey, side_e[1, k + 1]) - ey
@@ -314,6 +320,23 @@
         side_hz = side_h[2, k + 1] - side_step * (ey_dx + p2 - ex_dy - p3)
         side_h[0, k + 1], side_h[1, k + 1], side_h[2, k + 1] = side_hx, side_hy, side_hz
 
+    def tick(s, slot, k):
+        more = s < STEPS - 1
+        hdx, hgx, hdy, hgy = prof[0], prof[1], prof[2], prof[3]
+        edx, egx, edy, egy = prof[4], prof[5], prof[6], prof[7]
+        bdx, bgx = prof[8], prof[9]
+        prior = jnp.where(k > 0, k - 1, chunks)
+        wait_recv(0, slot, k)
+        wait_recv(1, slot, k)
+        wait_send(0, slot, k)
+
+        @pl.when(k > 0)
+        def _():
+            wait_send(1, slot, k - 1)
+
+        side_magnetic(slot, k)
+        edge_ex, edge_ez = side_e[0, k], side_e[2, k]
+        side_hx, side_hy, side_hz = side_h[0, k + 1], side_h[1, k + 1], side_h[2, k + 1]
         ey, ez = up_out[k, 0:size, :], up_out[k, size:2 * size, :]
         p1 = bdx * before_psi[0, k] + bgx * ez
         p2 = bdx * before_psi[1, k] + bgx * ey
@@ -323,13 +346,10 @@
         before[0, k], before[1, k] = hy, hz
         ey, ez = up_out[k, 2 * size:2 * size + 1, :], up_out[k, 2 * size + 1:2 * size + 2, :]
         factor = side_step[0:1] * (1.0 + bgx[0:1])
-        wait_recv(1, slot, k)
         before_h[0:size, :] = up_mask * (hy + down_in[slot, k, 0:size, :])
         before_h[size:2 * size, :] = up_mask * (hz + down_in[slot, k, size:2 * size, :])
         back_y = up_mask * (down_in[slot, k, 2 * size:2 * size + 1, :] + factor * ez)
         back_z = up_mask * (down_in[slot, k, 2 * size + 1:2 * size + 2, :] - factor * ey)
-
-        wait_send(0, slot, k)
 
         last_hx, last_hz, first_ex, first_ez = zero, zero, zero, zero
         below_hx, below_hy = h_s[0, k * size], h_s[1, k * size]
@@ -393,6 +413,7 @@
             ex, ey, ez = next_ex, next_ey, next_ez
         first_y[0, k] = first_ex
         first_y[1, k] = first_ez
+        below_main(prior)
 
         sdy, sgy = prof[14], prof[15]
         hx, hy, hz = side_hx, side_hy, side_hz
@@ -415,41 +436,49 @@
         up_out[k, 2 * size:2 * size + 1, :] = ey[0:1]
         up_out[k, 2 * size + 1:2 * size + 2, :] = ez[0:1]
 
+        below_side(prior)
+
         @pl.when(more)
         def _():
             start(0, 1 - slot, k)
 
-    def send_below(s, slot, k):
-        wait_send(1, slot, k)
-
-        @pl.when(s < STEPS - 1)
-        def _():
-            below(k)
-            start(1, 1 - slot, k)
+        @pl.when(jnp.logical_and(more, k > 0))
+        def _():
+            start(1, 1 - slot, k - 1)
 
     def step(s, carry):
         slot = lax.rem(s, 2)
-        for copy in mode_copies(s):
-            copy.start()
-
         def body(k, carry):
             tick(s, slot, k)
-
-            @pl.when(k > 0)
-            def _():
-                send_below(s, slot, k - 1)
-
             return carry
 
         lax.fori_loop(0, chunks, body, 0)
-        send_below(s, slot, chunks - 1)
+        wait_send(1, slot, chunks - 1)
+
+        @pl.when(s < STEPS - 1)
+        def _():
+            below_main(chunks - 1)
+            below_side(chunks - 1)
+            start(1, 1 - slot, chunks - 1)
+
+        @pl.when(s < STEPS - 1)
+        def _():
+            for copy in mode_copies(s):
+                copy.start()
+
+        @pl.when(s == STEPS - 2)
+        def _():
+            for copy in mode_copies(STEPS - 1):
+                copy.start()
+
         return carry
 
     lax.fori_loop(0, STEPS, step, 0)
     for side in range(2):
         @pl.when(sides[side][0])
         def _():
-            y_copy(side).wait_send()
+            for part_no in range(2):
+                y_copy(side, False, part_no).wait_send()
 
     count = snaps.shape[0] // nx
 
@@ -519,19 +548,24 @@
     exchange(near, lambda peer: total.at[own], total.at[own], back_send, back_recv)
 
 
-def write_kernel(e_s, h_s, total, e_out, h_out, proj_out, gram_out, sems):
+def write_kernel(e_s, h_s, total, e_out, h_out, proj_out, gram_out, proj, gram, sems):
     nz = e_out.shape[1]
-    store_e = pltpu.make_async_copy(e_s.at[:, pl.ds(0, nz)], e_out, sems.at[0])
-    store_h = pltpu.make_async_copy(h_s.at[:, pl.ds(1, nz)], h_out, sems.at[1])
-    store_e.start()
-    store_h.start()
-    n_all, count = proj_out.shape[1], gram_out.shape[1]
+    copies = [
+        pltpu.make_async_copy(e_s.at[:, pl.ds(0, nz)], e_out, sems.at[0]),
+        pltpu.make_async_copy(h_s.at[:, pl.ds(1, nz)], h_out, sems.at[1]),
+        pltpu.make_async_copy(proj, proj_out, sems.at[2]), pltpu.make_async_copy(gram, gram_out, sems.at[3]),
+    ]
+    copies[0].start()
+    copies[1].start()
+    n_all, count = proj.shape[1], gram.shape[1]
     share = total.shape[1]
     for k in range(total.shape[0]):
-        proj_out[k * share:(k + 1) * share, :] = total[k, :, 0:n_all]
-        gram_out[k * share:(k + 1) * share, :] = total[k, :, n_all:n_all + count]
-    store_e.wait()
-    store_h.wait()
+        proj[k * share:(k + 1) * share, :] = total[k, :, 0:n_all]
+        gram[k * share:(k + 1) * share, :] = total[k, :, n_all:n_all + count]
+    copies[2].start()
+    copies[3].start()
+    for copy in copies:
+        copy.wait()
 
 
 def shards(e_field, h_field, e_coef, basis, pml_width, snap_index):
@@ -553,13 +587,13 @@
         out_specs=[vmem, vmem, vmem],
         scratch_shapes=[
             pltpu.VMEM((nz, nx, ny), f32), pltpu.VMEM((8, nz, nx, ny), f32),
-            pltpu.VMEM((3, chunks + 1, nx, ny), f32), pltpu.VMEM((3, chunks + 1, nx, ny), f32),
-            pltpu.VMEM((chunks, nx, ny), f32), pltpu.VMEM((8, chunks, nx, ny), f32),
-            pltpu.VMEM((2, chunks, nx, ny), f32),
+            pltpu.VMEM((3, chunks + 2, nx, ny), f32), pltpu.VMEM((3, chunks + 2, nx, ny), f32),
+            pltpu.VMEM((chunks, nx, ny), f32), pltpu.VMEM((8, chunks + 1, nx, ny), f32),
+            pltpu.VMEM((2, chunks + 1, nx, ny), f32),
             pltpu.VMEM((2, 7, chunks // 2, nx, ny), f32), pltpu.VMEM((2, 7, chunks // 2, nx, ny), f32),
             pltpu.VMEM((chunks, 3 * size, ny), f32), pltpu.VMEM((2, chunks, 3 * size, ny), f32),
-            pltpu.VMEM((chunks, 3 * size, ny), f32), pltpu.VMEM((2, chunks, 3 * size, ny), f32),
-            pltpu.VMEM((3, chunks + 1, size, ny), f32), pltpu.VMEM((3, chunks, size, ny), f32),
+            pltpu.VMEM((chunks + 1, 3 * size, ny), f32), pltpu.VMEM((2, chunks, 3 * size, ny), f32),
+            pltpu.VMEM((3, chunks + 2, size, ny), f32), pltpu.VMEM((3, chunks + 1, size, ny), f32),
             pltpu.VMEM((2, chunks, size, ny), f32), pltpu.VMEM((2, chunks, size, ny), f32),
             pltpu.VMEM((2 * size, ny), f32),
             pltpu.VMEM((16, nx, ny), f32),
@@ -567,7 +601,7 @@
             pltpu.VMEM((2 * n_row, share, wide), f32), pltpu.VMEM((2 * n_row, share, wide), f32),
             pltpu.VMEM((n_col // 2, share, wide), f32),
             pltpu.SemaphoreType.DMA((4,)),
-            pltpu.SemaphoreType.DMA((2,)), pltpu.SemaphoreType.DMA((2,)),
+            pltpu.SemaphoreType.DMA((2, 2)), pltpu.SemaphoreType.DMA((2, 2)),
             pltpu.SemaphoreType.DMA((2, 2, chunks)), pltpu.SemaphoreType.DMA((2, 2, chunks)),
             pltpu.SemaphoreType.DMA((n_row - 1, STEPS)), pltpu.SemaphoreType.DMA((n_row - 1, STEPS)),
             pltpu.SemaphoreType.DMA((2 * n_row - 1,)), pltpu.SemaphoreType.DMA((2 * n_row - 1,)),
@@ -585,8 +619,10 @@
             jax.ShapeDtypeStruct((count, modes), f32), jax.ShapeDtypeStruct((count, count), f32),
         ],
         in_specs=[vmem, vmem, vmem],
-        out_specs=[any_space, any_space, vmem, vmem],
-        scratch_shapes=[pltpu.SemaphoreType.DMA((2,))],
+        out_specs=[any_space, any_space, any_space, any_space],
+        scratch_shapes=[
+            pltpu.VMEM((count, modes), f32), pltpu.VMEM((count, count), f32), pltpu.SemaphoreType.DMA((4,)),
+        ],
         compiler_params=pltpu.CompilerParams(vmem_limit_bytes=16_777_216),
     )(e_s, h_s, total)
 

time: 60 us -> 57.9 us (0.965)
  Pallas kernels: 59.2 us -> 57 us
    pallas_call x1, Pallas kernels: 57.4 us -> 55.9 us  [shards(): pl.pallas_call(functools.partial(step_kernel, n_row, n_col), out_shape=[h...]
    pallas_call x1, Pallas kernels: 1.78 us -> 1.18 us  [shards(): pl.pallas_call(write_kernel, out_shape=[jax.ShapeDtypeStruct(e_field.shap...]
where the time goes in v3:
time: 57.9 us; the launch traced here: 57.7 us
  Pallas kernels  57 us (98%)
  between operations  0.64 us (1%)
    pallas_call x1, Pallas kernels, shards(): pl.pallas_call(functools.partial(step_kernel, n_row, n_col), out_shape=[h...  55.9 us
    pallas_call x1, Pallas kernels, shards(): pl.pallas_call(write_kernel, out_shape=[jax.ShapeDtypeStruct(e_field.shap...  1.18 us

profile of v3, /device:TPU:0, one launch (start us, length us, event | category | flops | bytes accessed | tf_op | source)
XLA Modules:
  0.0 57.7 jit_solution(17299055144672705376)
XLA Ops:
  0.6 55.9 %shard_map.93 = (f32[3,65,8,128]{3,2,1,0:T(8,128)S(1)}, f32[3,65,8,128]{3,2,1,0:T(8,128)S(1)}, f32[8,8,256]{2,1,0:T(8,128)S(1)}) custom-call(s32[4]{0:T(128)} %width_ref.1, s32[64]{0:T(128)} %index_ref.1, f32[3,64,8,128]{3,2,1,0:T(8,128)} %e_in.1, f32[3,64,8,128]{3,2,1,0:T(8,128)} %h_in.1, f32[64,8,128]{2,1,0:T(8,128)} %coef_in.1, f32[32,32,128]{2,1,0:T(8,128)} %basis_in.1), custom_call_target="tpu_custom_call" | custom-call | tf_op jit(solution)/shard_map/pallas_call | solution.py:583
  56.5 1.2 %shard_map.94 = (f32[3,64,8,128]{3,2,1,0:T(8,128)}, f32[3,64,8,128]{3,2,1,0:T(8,128)}, f32[64,128]{1,0:T(8,128)}, f32[64,64]{1,0:T(8,128)}) custom-call(f32[3,65,8,128]{3,2,1,0:T(8,128)S(1)} %get-tuple-element.7.e_s, f32[3,65,8,128]{3,2,1,0:T(8,128)S(1)} %get-tuple-element.8.h_s, f32[8,8,256]{2,1,0:T(8,128)S(1)} %get-tuple-element.9.total), custom_call_target="tpu_custom_call" | custom-call | tf_op jit(solution)/shard_map/pallas_call | solution.py:615

commit v4 on v3

--- a/solution.py
+++ b/solution.py
@@ -62,7 +62,6 @@
     far = [{"row": row, "col": lax.rem(col + 2 * k, n_col)} for k in range(1, n_col // 2)]
     other = col - 1 + 2 * pair
     beside = jnp.logical_and(other >= 0, other < n_col)
-    part[...] = jnp.zeros_like(part)
     up_in[...] = jnp.zeros_like(up_in)
     down_in[...] = jnp.zeros_like(down_in)
     for side, there in enumerate((left, right)):
@@ -155,18 +154,17 @@
 
     sides = ((left, {"row": row, "col": col - 1}), (right, {"row": row, "col": col + 1}))
 
-    def y_copy(side, arriving, part):
-        parts = (pl.ds(0, 6), pl.ds(6, 1))[part]
+    def y_copy(side, arriving, q):
         a = 1 - side if arriving else side
         return pltpu.make_async_remote_copy(
-            src_ref=y_out.at[a, parts], dst_ref=y_in.at[1 - a, parts], send_sem=y_send.at[a, part],
-            recv_sem=y_recv.at[1 - a, part], device_id=sides[side][1], device_id_type=pl.DeviceIdType.MESH)
-
-    def y_wait(part):
+            src_ref=y_out.at[a, q], dst_ref=y_in.at[1 - a, q], send_sem=y_send.at[a, q],
+            recv_sem=y_recv.at[1 - a, q], device_id=sides[side][1], device_id_type=pl.DeviceIdType.MESH)
+
+    def y_each(act, q):
         for side in range(2):
             @pl.when(sides[side][0])
             def _():
-                y_copy(side, True, part).wait_recv()
+                act(side, q)
 
     load_e.wait()
     load_h.wait()
@@ -183,17 +181,17 @@
                 here = lax.div(lane, width) == i
                 first = jnp.where(here, pltpu.roll(value, i * width, 1) if i else value, first)
                 last = jnp.where(here, pltpu.roll(value, (i * width + width) % ny, 1) if (i + 1) % group else value, last)
-            y_out[0, c, q] = first
-            y_out[1, c, q] = last
+            y_out[0, q, c] = first
+            y_out[1, q, c] = last
         return carry
 
     lax.fori_loop(0, nz // group, pack_sides, 0)
     pl.semaphore_wait(barrier, len(near) + len(far) + beside.astype(jnp.int32))
-    for side in range(2):
-        @pl.when(sides[side][0])
-        def _():
-            for part_no in range(2):
-                y_copy(side, False, part_no).start()
+    def y_start(q, carry):
+        y_each(lambda side, q: y_copy(side, False, q).start(), q)
+        return carry
+
+    lax.fori_loop(0, nz // group, y_start, 0)
 
     def first_pack(k, carry):
         fx, fz = zero, zero
@@ -216,11 +214,9 @@
 
     lax.fori_loop(0, chunks, first_pack, 0)
 
-    y_wait(0)
-
-    def unpack(comps, q, carry):
-        for c in comps:
-            a, b = y_in[0, c, q], y_in[1, c, q]
+    def unpack(q):
+        for c in range(7):
+            a, b = y_in[0, q, c], y_in[1, q, c]
             values = jnp.where(on_left, a, pltpu.roll(b, half, 1)), jnp.where(on_left, pltpu.roll(a, half, 1), b)
             for i in range(2):
                 if c < 3:
@@ -229,9 +225,6 @@
                     side_h[c - 3, 2 * q + i + 1] = values[i]
                 else:
                     side_coef[2 * q + i] = values[i]
-        return carry
-
-    lax.fori_loop(0, nz // group, functools.partial(unpack, range(6)), 0)
 
     def z_after(here, after):
         return jnp.where(block == size - 1, pltpu.roll(after, half - width, 1), pltpu.roll(here, ny - width, 1))
@@ -274,18 +267,29 @@
         down_out[k, 2 * size:2 * size + 1, :] = hy[nx - 1:nx]
         down_out[k, 2 * size + 1:2 * size + 2, :] = hz[nx - 1:nx]
 
-    def first_send(k, carry):
-        up_out[k, 2 * size:2 * size + 1, :] = side_e[1, k, 0:1, :]
-        up_out[k, 2 * size + 1:2 * size + 2, :] = side_e[2, k, 0:1, :]
-        start(0, 0, k)
+    def first_below(k):
         below_main(k)
         below_side(k)
         start(1, 0, k)
-        return carry
-
-    lax.fori_loop(0, chunks, first_send, 0)
-    y_wait(1)
-    lax.fori_loop(0, nz // group, functools.partial(unpack, range(6, 7)), 0)
+
+    def first_send(q, carry):
+        y_each(lambda side, q: y_copy(side, True, q).wait_recv(), q)
+        unpack(q)
+        for i in range(2):
+            k = 2 * q + i
+            up_out[k, 2 * size:2 * size + 1, :] = side_e[1, k, 0:1, :]
+            up_out[k, 2 * size + 1:2 * size + 2, :] = side_e[2, k, 0:1, :]
+            start(0, 0, k)
+
+        @pl.when(q > 0)
+        def _():
+            first_below(2 * q - 1)
+
+        first_below(2 * q)
+        return carry
+
+    lax.fori_loop(0, chunks // 2, first_send, 0)
+    first_below(chunks - 1)
     piece = n_modes // STEPS
 
     def mode_copies(s):
@@ -474,11 +478,11 @@
         return carry
 
     lax.fori_loop(0, STEPS, step, 0)
-    for side in range(2):
-        @pl.when(sides[side][0])
-        def _():
-            for part_no in range(2):
-                y_copy(side, False, part_no).wait_send()
+    def y_end(q, carry):
+        y_each(lambda side, q: y_copy(side, False, q).wait_send(), q)
+        return carry
+
+    lax.fori_loop(0, nz // group, y_end, 0)
 
     count = snaps.shape[0] // nx
 
@@ -514,10 +518,13 @@
         g = lax.dot_general(a, a, dims, precision=lax.Precision.HIGHEST, preferred_element_type=jnp.float32)
         proj, gram = (p, g) if x == 0 else (proj + p, gram + g)
     gram = gram / float(nx * n_row * ny * n_col)
-    share = part.shape[1]
+    share = count // (2 * n_row)
+    fold = n_all // count
+    short = share // fold
     for k in range(part.shape[0]):
-        part[k, :, 0:n_all] = proj[k * share:(k + 1) * share]
-        part[k, :, n_all:n_all + count] = gram[k * share:(k + 1) * share]
+        part[k, 0:share, :] = proj[k * share:(k + 1) * share]
+        at = [k * share + m * short for m in range(fold)]
+        part[k, share:share + short, :] = jnp.concatenate([gram[m:m + short] for m in at], axis=1)
     own = 2 * row + pair
 
     def exchange(peers, src_of, dst, sends, recvs):
@@ -558,10 +565,13 @@
     copies[0].start()
     copies[1].start()
     n_all, count = proj.shape[1], gram.shape[1]
-    share = total.shape[1]
+    share = count // total.shape[0]
+    short = total.shape[1] - share
     for k in range(total.shape[0]):
-        proj[k * share:(k + 1) * share, :] = total[k, :, 0:n_all]
-        gram[k * share:(k + 1) * share, :] = total[k, :, n_all:n_all + count]
+        proj[k * share:(k + 1) * share, :] = total[k, 0:share, :]
+        for m in range(n_all // count):
+            at = k * share + m * short
+            gram[at:at + short, :] = total[k, share:share + short, m * count:(m + 1) * count]
     copies[2].start()
     copies[3].start()
     for copy in copies:
@@ -575,14 +585,13 @@
     f32 = jnp.float32
     size = ny // STEPS // 2
     chunks = nz // size
-    wide = modes + (count + 127) // 128 * 128
     any_space = pl.BlockSpec(memory_space=pltpu.HBM)
     smem, vmem = pl.BlockSpec(memory_space=pltpu.SMEM), pl.BlockSpec(memory_space=pltpu.VMEM)
     held = pltpu.VMEM((3, nz + 1, nx, ny), f32)
-    share = count // (2 * n_row)
+    lines = count // (2 * n_row) * (modes + count) // modes
     e_s, h_s, total = pl.pallas_call(
         functools.partial(step_kernel, n_row, n_col),
-        out_shape=[held, held, pltpu.VMEM((2 * n_row, share, wide), f32)],
+        out_shape=[held, held, pltpu.VMEM((2 * n_row, lines, modes), f32)],
         in_specs=[smem, smem, any_space, any_space, any_space, any_space],
         out_specs=[vmem, vmem, vmem],
         scratch_shapes=[
@@ -590,7 +599,7 @@
             pltpu.VMEM((3, chunks + 2, nx, ny), f32), pltpu.VMEM((3, chunks + 2, nx, ny), f32),
             pltpu.VMEM((chunks, nx, ny), f32), pltpu.VMEM((8, chunks + 1, nx, ny), f32),
             pltpu.VMEM((2, chunks + 1, nx, ny), f32),
-            pltpu.VMEM((2, 7, chunks // 2, nx, ny), f32), pltpu.VMEM((2, 7, chunks // 2, nx, ny), f32),
+            pltpu.VMEM((2, chunks // 2, 7, nx, ny), f32), pltpu.VMEM((2, chunks // 2, 7, nx, ny), f32),
             pltpu.VMEM((chunks, 3 * size, ny), f32), pltpu.VMEM((2, chunks, 3 * size, ny), f32),
             pltpu.VMEM((chunks + 1, 3 * size, ny), f32), pltpu.VMEM((2, chunks, 3 * size, ny), f32),
             pltpu.VMEM((3, chunks + 2, size, ny), f32), pltpu.VMEM((3, chunks + 1, size, ny), f32),
@@ -598,10 +607,10 @@
             pltpu.VMEM((2 * size, ny), f32),
             pltpu.VMEM((16, nx, ny), f32),
             pltpu.VMEM((modes * nx, ny), f32), pltpu.VMEM((count * nx, ny), f32),
-            pltpu.VMEM((2 * n_row, share, wide), f32), pltpu.VMEM((2 * n_row, share, wide), f32),
-            pltpu.VMEM((n_col // 2, share, wide), f32),
+            pltpu.VMEM((2 * n_row, lines, modes), f32), pltpu.VMEM((2 * n_row, lines, modes), f32),
+            pltpu.VMEM((n_col // 2, lines, modes), f32),
             pltpu.SemaphoreType.DMA((4,)),
-            pltpu.SemaphoreType.DMA((2, 2)), pltpu.SemaphoreType.DMA((2, 2)),
+            pltpu.SemaphoreType.DMA((2, chunks // 2)), pltpu.SemaphoreType.DMA((2, chunks // 2)),
             pltpu.SemaphoreType.DMA((2, 2, chunks)), pltpu.SemaphoreType.DMA((2, 2, chunks)),
             pltpu.SemaphoreType.DMA((n_row - 1, STEPS)), pltpu.SemaphoreType.DMA((n_row - 1, STEPS)),
             pltpu.SemaphoreType.DMA((2 * n_row - 1,)), pltpu.SemaphoreType.DMA((2 * n_row - 1,)),

time: 57.9 us -> 57.3 us (0.990)
    pallas_call x1, Pallas kernels: 55.9 us -> 55.3 us  [shards(): pl.pallas_call(functools.partial(step_kernel, n_row, n_col), out_shape=[h...]
where the time goes in v4:
time: 57.3 us; the launch traced here: 57.1 us
  Pallas kernels  56.5 us (99%)
  between operations  0.64 us (1%)
    pallas_call x1, Pallas kernels, shards(): pl.pallas_call(functools.partial(step_kernel, n_row, n_col), out_shape=[h...  55.3 us
    pallas_call x1, Pallas kernels, shards(): pl.pallas_call(write_kernel, out_shape=[jax.ShapeDtypeStruct(e_field.shap...  1.18 us

profile of v4, /device:TPU:0, one launch (start us, length us, event | category | flops | bytes accessed | tf_op | source)
XLA Modules:
  0.0 57.1 jit_solution(7430702866149159364)
XLA Ops:
  0.6 55.3 %shard_map.93 = (f32[3,65,8,128]{3,2,1,0:T(8,128)S(1)}, f32[3,65,8,128]{3,2,1,0:T(8,128)S(1)}, f32[8,12,128]{2,1,0:T(8,128)S(1)}) custom-call(s32[4]{0:T(128)} %width_ref.1, s32[64]{0:T(128)} %index_ref.1, f32[3,64,8,128]{3,2,1,0:T(8,128)} %e_in.1, f32[3,64,8,128]{3,2,1,0:T(8,128)} %h_in.1, f32[64,8,128]{2,1,0:T(8,128)} %coef_in.1, f32[32,32,128]{2,1,0:T(8,128)} %basis_in.1), custom_call_target="tpu_custom_call" | custom-call | tf_op jit(solution)/shard_map/pallas_call | solution.py:592
  55.9 1.2 %shard_map.94 = (f32[3,64,8,128]{3,2,1,0:T(8,128)}, f32[3,64,8,128]{3,2,1,0:T(8,128)}, f32[64,128]{1,0:T(8,128)}, f32[64,64]{1,0:T(8,128)}) custom-call(f32[3,65,8,128]{3,2,1,0:T(8,128)S(1)} %get-tuple-element.7.e_s, f32[3,65,8,128]{3,2,1,0:T(8,128)S(1)} %get-tuple-element.8.h_s, f32[8,12,128]{2,1,0:T(8,128)S(1)} %get-tuple-element.9.total), custom_call_target="tpu_custom_call" | custom-call | tf_op jit(solution)/shard_map/pallas_call | solution.py:624
